TPU v7x, 32 devices: a 4x4x1 block of a 4x4x8 slice. The times are simulated.
32 devices in a mesh: dp: 1 (over z), ep: 32 (over y, x, core).
Axes of the slice: x: 4, y: 4, z: 1, core: 2. Of those that a mesh axis runs over, the one named last changes fastest.
The devices are a block of a 4x4x8 slice.
Arguments:
- dy_home: bfloat16 [8192, 1024], P(('dp', 'ep'))
- topk_idx: int32 [8192, 8], P(('dp', 'ep'))
- slot_idx: int32 [8192, 8], P(('dp', 'ep'))
- gates: float32 [8192, 8], P(('dp', 'ep'))
- y_back: bfloat16 [8192, 8, 1024], P(('dp', 'ep'))
- x_disp: bfloat16 [32, 4096, 1024], P(('dp', 'ep'))
- h1_disp: bfloat16 [32, 4096, 512], P(('dp', 'ep'))
- h3_disp: bfloat16 [32, 4096, 512], P(('dp', 'ep'))
- w_gate: bfloat16 [32, 1024, 512], P('ep')
- w_up: bfloat16 [32, 1024, 512], P('ep')
- w_down: bfloat16 [32, 512, 1024], P('ep')
Outputs:
- output 1: bfloat16 [8192, 1024], P(('dp', 'ep'))
- output 2: float32 [8192, 8], P(('dp', 'ep'))
- output 3: float32 [32, 1024, 512], P(('dp', 'ep'))
- output 4: float32 [32, 1024, 512], P(('dp', 'ep'))
- output 5: float32 [32, 512, 1024], P(('dp', 'ep'))
All inputs are finite; a program needn't handle non-finite values.
Results may differ from a plain program's by a relative error of at most 0.0135394.
Values are sent between devices in bfloat16 or wider.
A program may use at most 768 MiB of HBM per device.

v0:
```python
import jax
import jax.numpy as jnp
from jax import lax
from jax.sharding import PartitionSpec as P


def gated_buffer(dy_rows, gates, flat_pos, rows_all):
    num_choice = flat_pos.size
    choice_of = jnp.full((rows_all,), num_choice, jnp.int32).at[flat_pos.reshape(-1)].set(
        jnp.arange(num_choice, dtype=jnp.int32), mode='drop')
    gate_pad = jnp.concatenate([gates.reshape(-1), jnp.zeros((1,), jnp.float32)])
    row_gate = gate_pad[choice_of]
    row_tok = jnp.minimum(choice_of // gates.shape[1], dy_rows.shape[0] - 1)
    row_dy = jnp.take(dy_rows, row_tok, axis=0)
    return (row_gate[:, None] * row_dy.astype(jnp.float32)).astype(jnp.bfloat16)


def expert_backward(dy_disp, x_disp, h_gate, h_up, w_gate, w_up, w_down):
    gate_f = h_gate.astype(jnp.float32)
    up_f = h_up.astype(jnp.float32)
    sig_gate = jax.nn.sigmoid(gate_f)
    silu_g = gate_f * sig_gate
    hidden_act = (silu_g * up_f).astype(jnp.bfloat16)
    d_act = jnp.einsum('erd,efd->erf', dy_disp, w_down, preferred_element_type=jnp.float32).astype(jnp.bfloat16).astype(jnp.float32)
    dh_gate = (d_act * up_f * sig_gate * (1.0 + gate_f * (1.0 - sig_gate))).astype(jnp.bfloat16)
    dh_up = (d_act * silu_g).astype(jnp.bfloat16)
    dw_down = jnp.einsum('erf,erd->efd', hidden_act, dy_disp, preferred_element_type=jnp.float32)
    dw_gate = jnp.einsum('erd,erf->edf', x_disp, dh_gate, preferred_element_type=jnp.float32)
    dw_up = jnp.einsum('erd,erf->edf', x_disp, dh_up, preferred_element_type=jnp.float32)
    dx_disp = (jnp.einsum('erf,edf->erd', dh_gate, w_gate, preferred_element_type=jnp.float32)
               + jnp.einsum('erf,edf->erd', dh_up, w_up, preferred_element_type=jnp.float32)).astype(jnp.bfloat16)
    return dx_disp, dw_gate, dw_up, dw_down


def solution(mesh):
    ep_size = mesh.shape['ep']
    tok_spec = P(('dp', 'ep'), None)
    buf_spec = P(('dp', 'ep'), None, None)
    expert_spec = P('ep', None, None)

    def device_step(dy_loc, topk_idx, slot_idx, gates, y_back, x_disp, h1_disp, h3_disp, w_gate, w_up, w_down):
        num_experts = w_gate.shape[0] * ep_size
        capacity = x_disp.shape[1] // ep_size
        d_model = dy_loc.shape[1]
        rows_all = num_experts * capacity
        d_gates = jnp.einsum('td,tjd->tj', dy_loc, y_back, preferred_element_type=jnp.float32)
        flat_pos = jnp.where(slot_idx >= 0, topk_idx * capacity + slot_idx, rows_all)
        send_buf = gated_buffer(dy_loc, gates, flat_pos, rows_all).reshape(num_experts, capacity, d_model)
        dy_disp = lax.all_to_all(send_buf, 'ep', 0, 1, tiled=True)
        dx_disp, dw_gate, dw_up, dw_down = expert_backward(dy_disp, x_disp, h1_disp, h3_disp, w_gate, w_up, w_down)
        dx_buf = lax.all_to_all(dx_disp, 'ep', 1, 0, tiled=True).reshape(rows_all, d_model)
        returned = jnp.take(dx_buf, flat_pos, axis=0, mode='fill', fill_value=0)
        dx_loc = jnp.sum(returned, axis=1, dtype=jnp.float32).astype(jnp.bfloat16)
        return dx_loc, d_gates, dw_gate, dw_up, dw_down

    return jax.shard_map(
        device_step, mesh=mesh,
        in_specs=(tok_spec, tok_spec, tok_spec, tok_spec, buf_spec, buf_spec, buf_spec, buf_spec,
                  expert_spec, expert_spec, expert_spec),
        out_specs=(tok_spec, tok_spec, buf_spec, buf_spec, buf_spec),
        check_vma=False)
```

profile of v0, /device:TPU:97, one launch (start us, length us, event | category | flops | bytes accessed | tf_op | source)
XLA Modules:
  0.0 453.5 jit_solution(17008846251013468706)
XLA Ops:
  0.6 0.8 compare_and_fusion
  1.5 0.1 copy.34
  1.6 0.1 reshape.119
  1.7 8.1 %scatter_custom_fusion = s32[4096]{0:T(1024)S(1)} fusion(s32[2048]{0:T(1024)S(1)} %bitcast.83, s32[2048]{0:T(1024)S(1)} %iota.3, s32[]{:T(128)} %constant.34.clone.1), kind=kCustom, calls=%fused_computation.61 | custom fusion | bytes 16388 | tf_op jit(solution)/shard_map/scatter | solution.py:9
  9.9 0.8 copy.33
  10.8 23.0 %gather_fusion = f32[4096]{0:T(1024)S(1)} fusion(f32[2049]{0:T(1024)S(1)} %pad_maximum_fusion, s32[4096]{0:T(1024)S(1)} %get-tuple-element.27), kind=kCustom, calls=%fused_computation | custom fusion | bytes 49152 | tf_op jit(solution)/shard_map/gather | solution.py:12
  33.9 18.2 %gather_fusion.1 = bf16[4096,1024]{1,0:T(8,128)(2,1)} fusion(bf16[256,1024]{1,0:T(8,128)(2,1)S(1)} %copy-done.2, s32[4096]{0:T(1024)S(1)} %get-tuple-element.28), kind=kCustom, calls=%fused_computation.1 | custom fusion | bytes 16793600 | tf_op jit(solution)/shard_map/jit(_take)/gather | solution.py:14
  52.1 5.1 %multiply_convert_fusion = bf16[32,128,1024]{2,1,0:T(8,128)(2,1)S(1)} fusion(bf16[32,128,1024]{2,1,0:T(8,128)(2,1)} %bitcast.78, f32[32,128]{1,0:T(8,128)S(1)} %bitcast.81, pred[32,128]{1,0:T(8,128)(4,1)S(1)} %and_bitcast_fusion), kind=kLoop, calls=%fused_computation.5 | loop fusion | flops 16777216 | bytes 16797696 | tf_op jit(solution)/shard_map/convert_element_type | solution.py:15
  57.3 111.2 %all_to_all.8 = bf16[32,128,1024]{2,1,0:T(8,128)(2,1)S(1)} all-to-all(bf16[32,128,1024]{2,1,0:T(8,128)(2,1)S(1)} %multiply_convert_fusion), channel_id=1, replica_groups=mesh['dp'=1,'ep'=32] {'ep'}, dimensions={0} | all-to-all | bytes 16777216 | tf_op jit(solution)/shard_map/all_to_all | solution.py:49
  168.5 9.5 %fusion.3 = (bf16[1,4096,512]{2,1,0:T(8,128)(2,1)}, bf16[1,4096,512]{2,1,0:T(8,128)(2,1)}) fusion(bf16[1,4096,512]{2,1,0:T(8,128)(2,1)S(1)} %copy-done.4, bf16[1,4096,512]{2,1,0:T(8,128)(2,1)S(1)} %copy-done.5, bf16[4096,1024]{1,0:T(8,128)(2,1)S(1)} %bitcast.79, bf16[1,512,1024]{2,1,0:T(8,128)(2,1)S(1)} %copy-done), kind=kOutput, calls=%fused_computation.15 | convolution fusion | flops 4324327424 | bytes 26214400 | tf_op jit(solution)/shard_map/erd,efd->erf/dot_general | solution.py:24
  178.0 10.4 %fusion.21 = f32[4096,1024]{1,0:T(8,128)} fusion(bf16[1,4096,512]{2,1,0:T(8,128)(2,1)} %get-tuple-element.29, bf16[1,1024,512]{2,1,0:T(8,128)(2,1)S(1)} %copy-done.6), kind=kOutput, calls=%fused_computation.35 | convolution fusion | flops 4294967296 | bytes 22020096 | tf_op jit(solution)/shard_map/erf,edf->erd/dot_general | solution.py:30
  188.5 11.8 %fusion.9 = bf16[1,4096,1024]{2,1,0:T(8,128)(2,1)} fusion(f32[4096,1024]{1,0:T(8,128)} %fusion.21, bf16[1,1024,512]{2,1,0:T(8,128)(2,1)S(1)} %copy-done.7, bf16[1,4096,512]{2,1,0:T(8,128)(2,1)} %get-tuple-element.30, bf16[1,4096,512]{2,1,0:T(8,128)(2,1)S(1)} %copy-done.5), kind=kOutput, calls=%fused_computation.21 | convolution fusion | flops 4320133120 | bytes 34603008 | tf_op jit(solution)/shard_map/erf,edf->erd/dot_general | solution.py:31
  200.3 15.5 %copy.47 = bf16[1,4096,1024]{2,0,1:T(2,128)(2,1)} copy(bf16[1,4096,1024]{2,1,0:T(8,128)(2,1)} %fusion.9) | data formatting | bytes 16777216 | tf_op jit(solution)/shard_map/convert_element_type | solution.py:31
  215.8 0.5 broadcast.56
  216.3 49.7 %reduce.1 = bf16[4096,1024]{1,0:T(8,128)(2,1)} reduce(bf16[4096,1,1024]{2,1,0:T(2,128)(2,1)} %bitcast.77, bf16[]{:T(256)} %broadcast.56), dimensions={1}, to_apply=%bitcast.72.reduce_sub_computation | reduce | bytes 16777218
  266.0 21.6 %reshape.170 = bf16[32,2,65536]{2,1,0:T(2,128)(2,1)} reshape(bf16[4096,1024]{1,0:T(8,128)(2,1)} %reduce.1) | data formatting | bytes 16777216
  287.6 4.8 %all-to-all-start.1 = ((bf16[32,2,65536]{2,1,0:T(2,128)(2,1)}), bf16[32,2,65536]{2,1,0:T(2,128)(2,1)}, u32[]{:S(2)}, u32[]{:S(2)}) async-start(bf16[32,2,65536]{2,1,0:T(2,128)(2,1)} %reshape.170), calls=%async_computation.1 | async-start | bytes 16777216 | tf_op jit(solution)/shard_map/all_to_all | solution.py:51
  292.4 0.2 copy.32
  292.6 0.1 copy.36
  292.8 0.1 reshape.148
  292.9 4.8 %fusion.37 = f32[256,1,8]{2,1,0:T(1,128)S(1)} fusion(bf16[256,8,1024]{2,1,0:T(8,128)(2,1)} %param.15, bf16[256,1024,1]{1,0,2:T(8,128)(2,1)S(1)} %bitcast.74), kind=kOutput, calls=%fused_computation.43 | convolution fusion | flops 4194304 | bytes 4726784 | tf_op jit(solution)/shard_map/td,tjd->tj/dot_general | solution.py:46
  297.7 0.7 copy.40
  298.4 8.2 %fusion.26 = f32[1,1024,512]{1,2,0:T(8,128)S(1)} fusion(bf16[1,4096,1024]{2,1,0:T(8,128)(2,1)} %param.16, bf16[1,4096,512]{2,1,0:T(8,128)(2,1)} %get-tuple-element.29), kind=kOutput, calls=%fused_computation.38 | convolution fusion | flops 4294967296 | bytes 14680064 | tf_op jit(solution)/shard_map/erd,erf->edf/dot_general | solution.py:28
  306.6 1.8 copy.37
  308.4 9.8 %fusion.31 = f32[1,1024,512]{1,2,0:T(8,128)S(1)} fusion(bf16[1,4096,1024]{2,1,0:T(8,128)(2,1)} %param.16, bf16[1,4096,512]{2,1,0:T(8,128)(2,1)} %get-tuple-element.30, bf16[1,4096,512]{2,1,0:T(8,128)(2,1)} %param.17), kind=kOutput, calls=%fused_computation.39 | convolution fusion | flops 4311744512 | bytes 18874368 | tf_op jit(solution)/shard_map/erd,erf->edf/dot_general | solution.py:29
  318.3 1.8 copy.38
  320.1 11.9 %fusion.23 = f32[1,512,1024]{2,1,0:T(8,128)} fusion(bf16[4096,1024]{1,0:T(8,128)(2,1)} %bitcast.80, bf16[1,4096,512]{2,1,0:T(8,128)(2,1)} %param.18, bf16[1,4096,512]{2,1,0:T(8,128)(2,1)} %param.17), kind=kOutput, calls=%fused_computation.37 | convolution fusion | flops 4311744512 | bytes 18874368 | tf_op jit(solution)/shard_map/erf,erd->efd/dot_general | solution.py:27
  332.0 65.6 %all-to-all-done.1 = bf16[32,2,65536]{2,1,0:T(2,128)(2,1)} async-done(((bf16[32,2,65536]{2,1,0:T(2,128)(2,1)}), bf16[32,2,65536]{2,1,0:T(2,128)(2,1)}, u32[]{:S(2)}, u32[]{:S(2)}) %all-to-all-start.1) | async-done | bytes 8388640 | tf_op jit(solution)/shard_map/all_to_all | solution.py:51
  397.6 23.4 %reshape.171 = bf16[4096,1,1024]{2,1,0:T(2,128)(2,1)} reshape(bf16[32,2,65536]{2,1,0:T(2,128)(2,1)} %all-to-all-done.1) | data formatting | bytes 16777216
  421.0 12.1 %copy.46 = bf16[1,4096,1024]{2,1,0:T(8,128)(2,1)} copy(bf16[1,4096,1024]{2,0,1:T(2,128)(2,1)} %bitcast.76) | data formatting | bytes 16777216
  433.1 15.4 %gather_fusion.2 = bf16[2048,1024]{1,0:T(8,128)(2,1)} fusion(bf16[4096,1024]{1,0:T(8,128)(2,1)} %bitcast.75, s32[2048]{0:T(1024)S(1)} %broadcast_clamp_fusion.1), kind=kCustom, calls=%fused_computation.2 | custom fusion | bytes 8396800 | tf_op jit(solution)/shard_map/jit(_take)/gather | solution.py:52
  448.6 4.9 %fusion.19 = bf16[256,1024]{1,0:T(8,128)(2,1)} fusion(bf16[2048,1024]{1,0:T(8,128)(2,1)} %gather_fusion.2, pred[256,8]{1,0:T(8,128)(4,1)S(1)} %copy.32), kind=kLoop, calls=%fused_computation.33 | loop fusion | flops 3932160 | bytes 4720640 | tf_op jit(solution)/shard_map/reduce_sum | solution.py:53
  (24 shorter events, 0.2 us)
Async XLA Ops:
  0.6 167.9 %copy-start = (bf16[1,512,1024]{2,1,0:T(8,128)(2,1)S(1)}, bf16[1,512,1024]{2,1,0:T(8,128)(2,1)}, u32[]{:S(2)}) copy-start(bf16[1,512,1024]{2,1,0:T(8,128)(2,1)} %param.21) | copy-start | bytes 3145732
  10.8 23.1 %copy-start.2 = (bf16[256,1024]{1,0:T(8,128)(2,1)S(1)}, bf16[256,1024]{1,0:T(8,128)(2,1)}, u32[]{:S(2)}) copy-start(bf16[256,1024]{1,0:T(8,128)(2,1)} %param.11) | copy-start | bytes 1572868
  57.2 111.3 %copy-start.4 = (bf16[1,4096,512]{2,1,0:T(8,128)(2,1)S(1)}, bf16[1,4096,512]{2,1,0:T(8,128)(2,1)}, u32[]{:S(2)}) copy-start(bf16[1,4096,512]{2,1,0:T(8,128)(2,1)} %param.18) | copy-start | bytes 12582916
  57.2 111.3 %copy-start.5 = (bf16[1,4096,512]{2,1,0:T(8,128)(2,1)S(1)}, bf16[1,4096,512]{2,1,0:T(8,128)(2,1)}, u32[]{:S(2)}) copy-start(bf16[1,4096,512]{2,1,0:T(8,128)(2,1)} %param.17) | copy-start | bytes 12582916
  168.5 9.5 %copy-start.3 = (bf16[32,128,1024]{2,1,0:T(8,128)(2,1)}, bf16[32,128,1024]{2,1,0:T(8,128)(2,1)S(1)}, u32[]{:S(2)}) copy-start(bf16[32,128,1024]{2,1,0:T(8,128)(2,1)S(1)} %all_to_all.8) | copy-start | bytes 25165828
  168.5 9.5 %copy-start.6 = (bf16[1,1024,512]{2,1,0:T(8,128)(2,1)S(1)}, bf16[1,1024,512]{2,1,0:T(8,128)(2,1)}, u32[]{:S(2)}) copy-start(bf16[1,1024,512]{2,1,0:T(8,128)(2,1)} %param.19) | copy-start | bytes 3145732
  178.0 10.5 %copy-start.7 = (bf16[1,1024,512]{2,1,0:T(8,128)(2,1)S(1)}, bf16[1,1024,512]{2,1,0:T(8,128)(2,1)}, u32[]{:S(2)}) copy-start(bf16[1,1024,512]{2,1,0:T(8,128)(2,1)} %param.20) | copy-start | bytes 3145732
  287.6 110.0 %all-to-all-start.1 = ((bf16[32,2,65536]{2,1,0:T(2,128)(2,1)}), bf16[32,2,65536]{2,1,0:T(2,128)(2,1)}, u32[]{:S(2)}, u32[]{:S(2)}) async-start(bf16[32,2,65536]{2,1,0:T(2,128)(2,1)} %reshape.170), calls=%async_computation.1 | async-start | bytes 16777216 | tf_op jit(solution)/shard_map/all_to_all | solution.py:51
  433.1 20.4 %copy-start.1 = (bf16[1,512,1024]{2,1,0:T(8,128)(2,1)S(1)}, bf16[1,512,1024]{2,1,0:T(8,128)(2,1)}, u32[]{:S(2)}) copy-start(bf16[1,512,1024]{2,1,0:T(8,128)(2,1)} %param.21) | copy-start | bytes 3145732
where the time goes:
time: 462 us; the launch traced here: 454 us
  local copies, waits for them, and re-layouts  144 us (31%)
  blocking collectives  111 us (24%)
  matrix products  66.5 us (14%)
  waiting for transfers between devices  65.6 us (14%)
  other arithmetic  60.7 us (13%)
  starting transfers between devices  4.81 us (1%)
    all_to_all x1, blocking collectives, device_step(): dy_disp = lax.all_to_all(send_buf, 'ep', 0, 1, tiled=True)  111 us
    all_to_all x1, waiting for transfers between devices, device_step(): lax.all_to_all(dx_disp, 'ep', 1, 0, tiled=True).reshape(rows_all, d_model)  65.6 us
    unnamed x23, local copies, waits for them, and re-layouts  62.1 us
    unnamed x1, other arithmetic  49.7 us
    gather x1, local copies, waits for them, and re-layouts, gated_buffer(): row_gate = gate_pad[choice_of]  23 us
    gather x1, local copies, waits for them, and re-layouts, gated_buffer(): row_dy = jnp.take(dy_rows, row_tok, axis=0)  18.2 us
    convert_element_type x1, local copies, waits for them, and re-layouts, expert_backward(): dx_disp = (jnp.einsum('erf,edf->erd', dh_gate, w_gate, preferred_element_...  15.5 us
    gather x1, local copies, waits for them, and re-layouts, device_step(): returned = jnp.take(dx_buf, flat_pos, axis=0, mode='fill', fill_value=0)  15.4 us
  transfers between devices with their start and end apart: 1, of which 1 were waited for; matrix products, arithmetic and copies ran while one was open for 9% of the time, Pallas kernels for 0%

commit v1 on v0

v1 whole, which is shorter than its diff:
```python
import functools

import jax
import jax.numpy as jnp
from jax import lax
from jax.experimental import pallas as pl
from jax.experimental.pallas import tpu as pltpu
from jax.sharding import PartitionSpec as P

F32 = jnp.float32
BF16 = jnp.bfloat16


def mm(a, b, dims):
    return lax.dot_general(a, b, (dims, ((), ())), preferred_element_type=F32)


def gated_rows(dy, slot, gate, capacity):
    rows = lax.broadcasted_iota(jnp.int32, (capacity, slot.shape[1]), 0).astype(F32)
    hit = rows == slot
    row_gate = jnp.sum(jnp.where(hit, gate, 0.0), axis=1, keepdims=True)
    picked = mm(jnp.where(hit, 1.0, 0.0).astype(BF16), dy, ((1,), (0,)))
    return (row_gate * picked).astype(BF16)


def expert_kernel(dy_ref, tab_ref, x_ref, h1_ref, h3_ref, w1_ref, w3_ref, w2_ref,
                  dx_ref, dw1_ref, dw3_ref, dw2_ref, dyd_ref, dh_ref):
    capacity = dx_ref.shape[0] // dy_ref.shape[0]
    ff = h1_ref.shape[1]

    @pl.when(pl.program_id(0) == 0)
    def _():
        dw1_ref[...] = jnp.zeros_like(dw1_ref)
        dw3_ref[...] = jnp.zeros_like(dw3_ref)
        dw2_ref[...] = jnp.zeros_like(dw2_ref)

    for i in range(dy_ref.shape[0]):
        dyd_ref[i * capacity:(i + 1) * capacity, :] = gated_rows(
            dy_ref[i], tab_ref[i, 0:1, :], tab_ref[i, 1:2, :], capacity)
    dyd = dyd_ref[...]
    d_act = mm(dyd, w2_ref[...], ((1,), (1,))).astype(BF16).astype(F32)
    g = h1_ref[...].astype(F32)
    u = h3_ref[...].astype(F32)
    sg = jax.nn.sigmoid(g)
    silu = g * sg
    act = (silu * u).astype(BF16)
    dh_ref[:, 0:ff] = (d_act * u * sg * (1.0 + g * (1.0 - sg))).astype(BF16)
    dh_ref[:, ff:2 * ff] = (d_act * silu).astype(BF16)
    dw2_ref[...] += mm(act, dyd, ((0,), (0,)))
    dh1 = dh_ref[:, 0:ff]
    dh3 = dh_ref[:, ff:2 * ff]
    dw1_ref[...] += mm(x_ref[...], dh1, ((0,), (0,)))
    dw3_ref[...] += mm(x_ref[...], dh3, ((0,), (0,)))
    dx_ref[...] = (mm(dh1, w1_ref[...], ((1,), (1,))) + mm(dh3, w3_ref[...], ((1,), (1,)))).astype(BF16)


def combine_kernel(slot_ref, rows_ref, dx_ref, acc_ref):
    capacity = rows_ref.shape[1]
    step = pl.program_id(0)

    @pl.when(step == 0)
    def _():
        acc_ref[...] = jnp.zeros_like(acc_ref)

    rows = lax.broadcasted_iota(jnp.int32, (capacity, slot_ref.shape[2]), 0).astype(F32)
    for i in range(rows_ref.shape[0]):
        hit = jnp.where(rows == slot_ref[i], 1.0, 0.0).astype(BF16)
        acc_ref[...] += mm(hit, rows_ref[i], ((0,), (0,)))

    @pl.when(step == pl.num_programs(0) - 1)
    def _():
        dx_ref[...] = acc_ref[...].astype(BF16)


def dgates_kernel(dy_ref, yb_ref, out_ref):
    out_ref[...] = jnp.sum(dy_ref[...].astype(F32)[:, None, :] * yb_ref[...].astype(F32), axis=2)


def solution(mesh):
    ep_size = mesh.shape['ep']
    tok_spec = P(('dp', 'ep'), None)
    buf_spec = P(('dp', 'ep'), None, None)
    expert_spec = P('ep', None, None)

    def device_step(dy, topk_idx, slot_idx, gates, y_back, x_disp, h1_disp, h3_disp, w_gate, w_up, w_down):
        capacity = x_disp.shape[1] // ep_size
        tokens, d = dy.shape
        top = gates.shape[1]
        ff = w_gate.shape[2]
        num_experts = w_gate.shape[0] * ep_size
        pair = 2
        rows = pair * capacity

        hit = topk_idx[None, :, :] == jnp.arange(num_experts, dtype=jnp.int32)[:, None, None]
        slot_of = (jnp.sum(jnp.where(hit, slot_idx[None] + 1, 0), axis=2) - 1).astype(F32)
        gate_of = jnp.sum(jnp.where(hit, gates[None], 0.0), axis=2)
        tab = lax.all_to_all(jnp.stack([slot_of, gate_of], axis=1), 'ep', 0, 0, tiled=True)
        dy_all = lax.all_gather(dy, 'ep', axis=0, tiled=False)

        params = pltpu.CompilerParams(vmem_limit_bytes=56 * 2 ** 20)
        tb = 32
        d_gates = pl.pallas_call(
            dgates_kernel, grid=(tokens // tb,),
            in_specs=[pl.BlockSpec((tb, d), lambda i: (i, 0)), pl.BlockSpec((tb, top, d), lambda i: (i, 0, 0))],
            out_specs=pl.BlockSpec((tb, top), lambda i: (i, 0)),
            out_shape=jax.ShapeDtypeStruct((tokens, top), F32), name='dgates',
            cost_estimate=pl.CostEstimate(flops=2 * tokens * top * d, bytes_accessed=2 * tokens * top * d, transcendentals=0),
        )(dy, y_back)

        const = lambda *shape: pl.BlockSpec(shape, lambda i: (0,) * len(shape))
        dx_rows, dw1, dw3, dw2 = pl.pallas_call(
            expert_kernel, grid=(ep_size // pair,),
            in_specs=[pl.BlockSpec((pair, tokens, d), lambda i: (i, 0, 0)),
                      pl.BlockSpec((pair, 2, tokens), lambda i: (i, 0, 0)),
                      pl.BlockSpec((rows, d), lambda i: (i, 0)),
                      pl.BlockSpec((rows, ff), lambda i: (i, 0)),
                      pl.BlockSpec((rows, ff), lambda i: (i, 0)),
                      const(d, ff), const(d, ff), const(ff, d)],
            out_specs=[pl.BlockSpec((rows, d), lambda i: (i, 0)), const(d, ff), const(d, ff), const(ff, d)],
            out_shape=[jax.ShapeDtypeStruct((ep_size * capacity, d), BF16),
                       jax.ShapeDtypeStruct((d, ff), F32), jax.ShapeDtypeStruct((d, ff), F32),
                       jax.ShapeDtypeStruct((ff, d), F32)],
            scratch_shapes=[pltpu.VMEM((rows, d), BF16), pltpu.VMEM((rows, 2 * ff), BF16)],
            compiler_params=params, name='experts',
        )(dy_all, tab, x_disp[0], h1_disp[0], h3_disp[0], w_gate[0], w_up[0], w_down[0])

        back = lax.all_to_all(dx_rows.reshape(ep_size, capacity, d), 'ep', 0, 0, tiled=True)
        eb = 4
        dx = pl.pallas_call(
            combine_kernel, grid=(num_experts // eb,),
            in_specs=[pl.BlockSpec((eb, 1, tokens), lambda i: (i, 0, 0)),
                      pl.BlockSpec((eb, capacity, d), lambda i: (i, 0, 0))],
            out_specs=const(tokens, d),
            out_shape=jax.ShapeDtypeStruct((tokens, d), BF16),
            scratch_shapes=[pltpu.VMEM((tokens, d), F32)],
            compiler_params=params, name='combine',
        )(slot_of[:, None, :], back)
        return dx, d_gates, dw1[None], dw3[None], dw2[None]

    return jax.shard_map(
        device_step, mesh=mesh,
        in_specs=(tok_spec, tok_spec, tok_spec, tok_spec, buf_spec, buf_spec, buf_spec, buf_spec,
                  expert_spec, expert_spec, expert_spec),
        out_specs=(tok_spec, tok_spec, buf_spec, buf_spec, buf_spec),
        check_vma=False)
```

time: 462 us -> 256 us (0.55)
  the two profiles are of different devices: /device:TPU:97 before, /device:TPU:103 now
where the time goes in v1:
time: 256 us
  waiting for transfers between devices  162 us (63%)
  Pallas kernels  57.3 us (22%)
  between operations  14.1 us (6%)
  blocking collectives  13.4 us (5%)
  starting transfers between devices  4.55 us (2%)
    all_to_all x1, waiting for transfers between devices, device_step(): lax.all_to_all(dx_rows.reshape(ep_size, capacity, d), 'ep', 0, 0, tiled=T...  105 us
    all_gather x1, waiting for transfers between devices, device_step(): dy_all = lax.all_gather(dy, 'ep', axis=0, tiled=False)  56.5 us
    pallas_call x1, Pallas kernels, device_step(): pl.pallas_call(expert_kernel, grid=(ep_size // pair,), in_specs=[pl.Block...  40.9 us
    all_to_all x1, blocking collectives, device_step(): lax.all_to_all(jnp.stack([slot_of, gate_of], axis=1), 'ep', 0, 0, tiled=T...  13.4 us
    pallas_call x1, Pallas kernels, device_step(): pl.pallas_call(combine_kernel, grid=(num_experts // eb,), in_specs=[pl.Bl...  9.78 us
    pallas_call x1, Pallas kernels, device_step(): pl.pallas_call(dgates_kernel, grid=(tokens // tb,), in_specs=[pl.BlockSpe...  6.62 us
  transfers between devices with their start and end apart: 2, of which 2 were waited for; matrix products, arithmetic and copies ran while one was open for 2% of the time, Pallas kernels for 3%

profile of v1, /device:TPU:103, one launch (start us, length us, event | category | flops | bytes accessed | tf_op | source)
XLA Modules:
  0.0 255.6 jit_solution(14273146102997497057)
XLA Ops:
  7.2 0.1 all-gather.3.cloned.1.call-start
  7.2 0.7 all-gather.3.cloned.1.call-update
  8.0 0.7 broadcast_add_fusion
  8.7 0.8 select_reduce_fusion.1
  9.5 0.0 copy-start
  9.5 0.8 select_reduce_fusion
  10.3 0.1 pad_maximum_fusion
  10.4 13.4 %all_to_all.10.tab_ref = f32[32,2,256]{2,1,0:T(2,128)} all-to-all(f32[32,2,256]{2,1,0:T(2,128)S(1)} %pad_maximum_fusion), channel_id=1, replica_groups=mesh['dp'=1,'ep'=32] {'ep'}, dimensions={0} | all-to-all | bytes 131072 | tf_op jit(solution)/shard_map/all_to_all | solution.py:97
  23.8 56.5 %all-gather.3.cloned.1.call-done = bf16[8192,1024]{1,0:T(8,128)(2,1)} async-done(((bf16[256,1024]{1,0:T(8,128)(2,1)}), bf16[8192,1024]{1,0:T(8,128)(2,1)}) %all-gather.3.cloned.1.call-update) | async-done | bytes 16777232 | tf_op jit(solution)/shard_map/all_gather | solution.py:98
  80.4 40.9 %experts.1 = (bf16[4096,1024]{1,0:T(8,128)(2,1)}, f32[1024,512]{1,0:T(8,128)}, f32[1024,512]{1,0:T(8,128)}, f32[512,1024]{1,0:T(8,128)}) custom-call(bf16[32,256,1024]{2,1,0:T(8,128)(2,1)} %bitcast.11, f32[32,2,256]{2,1,0:T(2,128)} %all_to_all.10.tab_ref, bf16[4096,1024]{1,0:T(8,128)(2,1)} %bitcast.13, bf16[4096,512]{1,0:T(8,128)(2,1)} %bitcast.14, ...), custom_call_target="tpu_custom_call" | custom-call | tf_op jit(solution)/shard_map/experts/pallas_call | solution.py:111
  121.3 0.0 copy-done
  121.3 4.5 %all-to-all-start.1 = ((bf16[32,128,1024]{2,1,0:T(8,128)(2,1)}), bf16[32,128,1024]{2,1,0:T(8,128)(2,1)}, u32[]{:S(2)}, u32[]{:S(2)}) async-start(bf16[32,128,1024]{2,1,0:T(8,128)(2,1)} %bitcast.12), calls=%async_computation.1 | async-start | bytes 16777216 | tf_op jit(solution)/shard_map/all_to_all | solution.py:127
  125.8 6.6 %dgates.1 = f32[256,8]{1,0:T(8,128)} custom-call(bf16[256,1024]{1,0:T(8,128)(2,1)} %dy_ref.1, bf16[256,8,1024]{2,1,0:T(8,128)(2,1)} %yb_ref.1), custom_call_target="tpu_custom_call" | custom-call | flops 4194304 | bytes 4194304 | tf_op jit(solution)/shard_map/dgates/pallas_call | solution.py:102
  132.4 1.6 copy.20
  134.0 105.0 %all-to-all-done.1.rows_ref = bf16[32,128,1024]{2,1,0:T(8,128)(2,1)} async-done(((bf16[32,128,1024]{2,1,0:T(8,128)(2,1)}), bf16[32,128,1024]{2,1,0:T(8,128)(2,1)}, u32[]{:S(2)}, u32[]{:S(2)}) %all-to-all-start.1) | async-done | bytes 8388640 | tf_op jit(solution)/shard_map/all_to_all | solution.py:127
  238.9 9.8 %combine.1 = bf16[256,1024]{1,0:T(8,128)(2,1)} custom-call(f32[32,1,256]{2,1,0:T(1,128)} %copy-done, bf16[32,128,1024]{2,1,0:T(8,128)(2,1)} %all-to-all-done.1.rows_ref), custom_call_target="tpu_custom_call" | custom-call | tf_op jit(solution)/shard_map/combine/pallas_call | solution.py:129
  (3 shorter events, 0.1 us)
Async XLA Ops:
  7.2 73.2 %all-gather.3.cloned.1.call-start = ((), (), s32[]{:S(2)}) async-start(), calls=%async_computation.2 | async-start | bytes 17301504 | tf_op jit(solution)/shard_map/all_gather | solution.py:98
  9.5 111.8 %copy-start = (f32[32,1,256]{2,1,0:T(1,128)}, f32[32,1,256]{2,1,0:T(1,128)S(1)}, u32[]{:S(2)}) copy-start(f32[32,1,256]{2,1,0:T(1,128)S(1)} %convert_element_type.14.slot_ref) | copy-start | bytes 98308
  121.3 117.6 %all-to-all-start.1 = ((bf16[32,128,1024]{2,1,0:T(8,128)(2,1)}), bf16[32,128,1024]{2,1,0:T(8,128)(2,1)}, u32[]{:S(2)}, u32[]{:S(2)}) async-start(bf16[32,128,1024]{2,1,0:T(8,128)(2,1)} %bitcast.12), calls=%async_computation.1 | async-start | bytes 16777216 | tf_op jit(solution)/shard_map/all_to_all | solution.py:127
Sparse Core Ops, SparseCore 0:
  10.1 70.2 all-gather.2

commit v2 on v0

v2 whole, which is shorter than its diff:
```python
import functools
import math

import jax
import jax.numpy as jnp
from jax import lax
from jax.experimental import pallas as pl
from jax.experimental.pallas import tpu as pltpu
from jax.sharding import PartitionSpec as P

F32 = jnp.float32
BF16 = jnp.bfloat16

ORDER = ((2, 2), (2, 1), (1, 2), (2, 3), (3, 2), (2, 0), (0, 2),
         (1, 1), (1, 3), (3, 1), (1, 0), (0, 1), (3, 3), (3, 0), (0, 3), (0, 0))
SUMS = ((8, 1, 2), (9, 0, 2), (13, 1, 1), (14, 0, 1), (16, 1, 3), (17, 0, 3), (18, 1, 0), (19, 0, 0))
RELAY_LAG = 2
SUM_RELAYS = ((12, 1), (13, 0))
STEPS = 20


def mm(a, b, dims):
    return lax.dot_general(a, b, (dims, ((), ())), preferred_element_type=F32)


def pick(k, values):
    out = jnp.int32(values[0])
    for i, v in enumerate(values[1:], 1):
        out = jnp.where(k == i, jnp.int32(v), out)
    return out


def kernel_body(side, capacity, dy_ref, tab_in, x_ref, h1_ref, h3_ref, w1_ref, w3_ref, w2_ref,
                dx_ref, dw1_ref, dw3_ref, dw2_ref,
                dyall, tab, w1, w3, w2, dw1, dw3, dw2, xb, h1b, h3b, dyd, dh, dxs, rcv, hitb,
                psend, pown, precv, prelay,
                load_sem, w_sem, in_sem, out_sem, ag_send, ag_recv, ag_recv2, tb_send, tb_recv, tb_recv2,
                r_send, r_recv, rl_send, p_send, p_recv, pl_send, pl_recv):
    tokens = dyall.shape[2]
    top = tab.shape[1] // 2
    half = dyall.shape[3]
    ff = h1b.shape[2]
    rows = 2 * capacity
    piece = tokens // 2
    row_len = 2 * side
    me = lax.axis_index('ep')
    core = me % 2
    x = (me // 2) % side
    y = me // (2 * side)
    far = side // 2

    def wrap(v):
        return (v + side) % side

    def block(bx, by):
        return by * side + bx

    def device(bx, by, c):
        return {'ep': block(bx, by) * 2 + c}

    def chip(f, r1, r2):
        return (wrap(x + r1), wrap(y + r2)) if f == 0 else (wrap(x + r2), wrap(y + r1))

    loads = [pltpu.make_async_copy(dy_ref.at[:, pl.ds(f * half, half)], dyall.at[me, f], load_sem.at[f]) for f in (0, 1)]
    loads.append(pltpu.make_async_copy(tab_in, tab.at[me], load_sem.at[2]))
    wloads = [pltpu.make_async_copy(a, b, w_sem.at[i]) for i, (a, b) in enumerate(((w1_ref, w1), (w3_ref, w3), (w2_ref, w2)))]
    for cp in loads + wloads:
        cp.start()

    def stream(k):
        b = block(wrap(x + pick(k, [o[0] for o in ORDER])), wrap(y + pick(k, [o[1] for o in ORDER])))
        s = k % 2
        src = pl.ds(b * rows, rows)
        return [pltpu.make_async_copy(x_ref.at[src], xb.at[s], in_sem.at[s, 0]),
                pltpu.make_async_copy(h1_ref.at[src], h1b.at[s], in_sem.at[s, 1]),
                pltpu.make_async_copy(h3_ref.at[src], h3b.at[s], in_sem.at[s, 2])]

    for cp in stream(jnp.int32(0)):
        cp.start()

    barrier = pltpu.get_barrier_semaphore()
    for c in (0, 1):
        for bx, by in ((wrap(x + 1), y), (wrap(x - 1), y), (x, wrap(y + 1)), (x, wrap(y - 1))):
            pl.semaphore_signal(barrier, inc=1, device_id=device(bx, by, c))
    pl.semaphore_signal(barrier, inc=1, device_id=device(x, y, 1 - core))
    pl.semaphore_wait(barrier, 9)

    def gather_copy(f, p, r1, r2, axis, sign):
        bx, by = chip(f, r1, r2)
        home = block(bx, by) * 2 + core
        src = dyall.at[home, f, pl.ds(p * piece, piece)]
        if axis is None:
            dev, rs, ts = device(x, y, 1 - core), ag_recv2, tb_recv2
        else:
            nx, ny = chip(f, sign, 0) if axis == 0 else chip(f, 0, sign)
            dev, rs, ts = device(nx, ny, core), ag_recv, tb_recv
        out = [pltpu.make_async_remote_copy(src, src, ag_send, rs.at[block(bx, by), f, p], device_id=dev)]
        if f == 0:
            t = tab.at[home, pl.ds(p * top, top)]
            out.append(pltpu.make_async_remote_copy(t, t, tb_send, ts.at[block(bx, by), p], device_id=dev))
        return out

    def send(f, p, r1, r2, axis, sign=0):
        for cp in gather_copy(f, p, r1, r2, axis, sign):
            cp.start()

    def arrived(f, p, r1, r2):
        for cp in gather_copy(f, p, r1, r2, 0, 1):
            cp.wait_recv()

    for cp in loads:
        cp.wait()
    for axis in (0, 1):
        for f in (0, 1):
            for p, sign in ((0, 1), (1, -1), (1, 1), (0, -1)):
                send(f, p, 0, 0, axis, sign)
    for f in (0, 1):
        for p in (0, 1):
            send(f, p, 0, 0, None)

    def second_axis(f, p, r1):
        send(f, p, r1, 0, 1, 1)
        send(f, p, r1, 0, 1, -1)
        send(f, p, r1, 0, None)

    def first_near():
        for f in (0, 1):
            for p, r in ((0, -1), (1, 1)):
                arrived(f, p, r, 0)
                send(f, p, r, 0, 0, -r)
                second_axis(f, p, r)
        for f in (0, 1):
            for p, r in ((1, -1), (0, 1)):
                arrived(f, p, r, 0)
                second_axis(f, p, r)

    def first_far():
        for f in (0, 1):
            for p in (0, 1):
                arrived(f, p, far, 0)
                second_axis(f, p, far)

    def second_near(r1):
        for f in (0, 1):
            for p, r in ((0, -1), (1, 1)):
                arrived(f, p, r1, r)
                send(f, p, r1, r, 1, -r)
                send(f, p, r1, r, None)
        for f in (0, 1):
            for p, r in ((1, -1), (0, 1)):
                arrived(f, p, r1, r)
                send(f, p, r1, r, None)

    def second_far(r1):
        for f in (0, 1):
            for p in (0, 1):
                arrived(f, p, r1, far)
                send(f, p, r1, far, None)

    first_near()
    dw1[...] = jnp.zeros_like(dw1)
    dw3[...] = jnp.zeros_like(dw3)
    dw2[...] = jnp.zeros_like(dw2)
    second_near(0)
    first_far()
    second_far(0)
    second_near(-1)
    second_near(1)
    second_near(far)
    second_far(-1)
    second_far(1)
    second_far(far)

    def plane(b, carry):
        home = b * 2 + 1 - core
        for f in (0, 1):
            for p in (0, 1):
                src = dyall.at[home, f, pl.ds(p * piece, piece)]
                pltpu.make_async_copy(src, src, ag_recv2.at[b, f, p]).wait()
        for p in (0, 1):
            t = tab.at[home, pl.ds(p * top, top)]
            pltpu.make_async_copy(t, t, tb_recv2.at[b, p]).wait()
        return carry

    lax.fori_loop(0, side * side, plane, 0)
    for cp in wloads:
        cp.wait()

    def compute(k, bx, by):
        s = k % 2
        for cp in stream(k):
            cp.wait()

        @pl.when(k + 1 < len(ORDER))
        def _():
            for cp in stream(k + 1):
                cp.start()

        slot_row = lax.broadcasted_iota(jnp.int32, (capacity, tokens), 0).astype(F32)
        base = (me * capacity).astype(F32)
        for i in (0, 1):
            home = block(bx, by) * 2 + i
            rel = tab[home, 0:top, :] - base
            mine = (rel >= 0.0) & (rel < float(capacity))
            slot = jnp.max(jnp.where(mine, rel, -1.0), axis=0, keepdims=True)
            gate = jnp.sum(jnp.where(mine, tab[home, top:2 * top, :], 0.0), axis=0, keepdims=True)
            hit = slot_row == slot
            row_gate = jnp.sum(jnp.where(hit, gate, 0.0), axis=1, keepdims=True)
            hit = jnp.where(hit, 1.0, 0.0).astype(BF16)
            for f in (0, 1):
                picked = mm(hit, dyall[home, f], ((1,), (0,)))
                dyd[i * capacity:(i + 1) * capacity, f * half:(f + 1) * half] = (row_gate * picked).astype(BF16)
        dyv = dyd[...]
        d_act = mm(dyv, w2[...], ((1,), (1,))).astype(BF16).astype(F32)
        g = h1b[s].astype(F32)
        u = h3b[s].astype(F32)
        sg = jax.nn.sigmoid(g)
        silu = g * sg
        act = (silu * u).astype(BF16)
        dh[:, 0:ff] = (d_act * u * sg * (1.0 + g * (1.0 - sg))).astype(BF16)
        dh[:, ff:2 * ff] = (d_act * silu).astype(BF16)
        dh1 = dh[:, 0:ff]
        dh3 = dh[:, ff:2 * ff]
        for f in (0, 1):
            cols = pl.ds(f * half, half)
            d_x = (mm(dh1, w1[cols, :], ((1,), (1,))) + mm(dh3, w3[cols, :], ((1,), (1,)))).astype(BF16)
            for i in (0, 1):
                dxs[f, block(bx, by) * 2 + i] = d_x[i * capacity:(i + 1) * capacity, :]
        dw2[...] += mm(act, dyv, ((0,), (0,)))
        dw1[...] += mm(xb[s], dh1, ((0,), (0,)))
        dw3[...] += mm(xb[s], dh3, ((0,), (0,)))

    def target(f, sign, c):
        return device(wrap(x + sign), y, c) if f == 0 else device(x, wrap(y + sign), c)

    def send_rows(k, bx, by):
        for f in (0, 1):
            d = pick(k, [o[f] for o in ORDER])
            pos = x if f == 0 else y
            other = by if f == 0 else bx
            slot_near = other * row_len + pos * 2 + core
            for cc in (0, 1):
                home = block(bx, by) * 2 + cc
                same = core == cc
                local = (d == 0) & same

                @pl.when(local)
                def _():
                    rcv[f, slot_near] = dxs[f, home]

                @pl.when(jnp.logical_not(local))
                def _():
                    plus = (d == 1) | ((d == far) & same)
                    sign = jnp.where(d == 0, 0, jnp.where(plus, 1, -1))
                    slot = jnp.where(d == far, side * row_len + jnp.where(same, 0, side) + other, slot_near)
                    pltpu.make_async_remote_copy(dxs.at[f, home], rcv.at[f, slot], r_send, r_recv.at[f, slot],
                                                 device_id=target(f, sign, cc)).start()

    def relay_rows(f, other):
        pos = x if f == 0 else y
        for sign in (1, -1):
            slot_in = side * row_len + (0 if sign == 1 else side) + other
            src_core = core if sign == 1 else 1 - core
            slot_out = other * row_len + wrap(pos - sign) * 2 + src_core
            cp = pltpu.make_async_remote_copy(rcv.at[f, slot_in], rcv.at[f, slot_out], rl_send,
                                              r_recv.at[f, slot_in], device_id=target(f, sign, core))
            cp.wait_recv()
            pltpu.make_async_remote_copy(rcv.at[f, slot_in], rcv.at[f, slot_out], rl_send,
                                         r_recv.at[f, slot_out], device_id=target(f, sign, core)).start()

    def sums(f, d):
        pos = x if f == 0 else y
        hx, hy = (x, wrap(y + d)) if f == 0 else (wrap(x + d), y)
        other = hy if f == 0 else hx
        home = block(hx, hy) * 2 + core
        code = tab[home, 0:top, :]
        slot_row = lax.broadcasted_iota(jnp.int32, (capacity, tokens), 0).astype(F32)
        for s in range(row_len):
            @pl.when(pos * 2 + core != s)
            def _():
                ref = rcv.at[f, other * row_len + s]
                pltpu.make_async_copy(ref, ref, r_recv.at[f, other * row_len + s]).wait()

            e = y * row_len + s if f == 0 else ((s // 2) * side + x) * 2 + s % 2
            rel = code - (e * capacity).astype(F32)
            slot = jnp.max(jnp.where((rel >= 0.0) & (rel < float(capacity)), rel, -1.0), axis=0, keepdims=True)
            hitb[s * capacity:(s + 1) * capacity, :] = jnp.where(slot_row == slot, 1.0, 0.0).astype(BF16)
        data = rcv[f, pl.ds(other * row_len, row_len)].reshape(row_len * capacity, half)
        return mm(hitb[...], data, ((0,), (0,)))

    def send_sums(f, d):
        axis = 1 - f
        if d == far:
            for i, sign in ((0, 1), (1, -1)):
                pltpu.make_async_remote_copy(psend.at[f, d - 1, pl.ds(i * piece, piece)], prelay.at[f, i], p_send,
                                             pl_recv.at[f, i], device_id=target(axis, sign, core)).start()
        else:
            sign = 1 if d == 1 else -1
            pltpu.make_async_remote_copy(psend.at[f, d - 1], precv.at[f, d - 1], p_send, p_recv.at[f, d - 1],
                                         device_id=target(axis, sign, core)).start()

    def far_sum(f, i):
        return precv.at[f, far - 1, pl.ds(i * piece, piece)], p_recv.at[f, far - 1 if i == 0 else side - 1]

    def relay_sums(f):
        for i, sign in ((0, 1), (1, -1)):
            src = prelay.at[f, i]
            pltpu.make_async_copy(src, src, pl_recv.at[f, i]).wait()
            dst, sem = far_sum(f, i)
            pltpu.make_async_remote_copy(src, dst, pl_send, sem, device_id=target(1 - f, sign, core)).start()

    def step(k, carry):
        @pl.when(k < len(ORDER))
        def _():
            bx = wrap(x + pick(k, [o[0] for o in ORDER]))
            by = wrap(y + pick(k, [o[1] for o in ORDER]))
            compute(k, bx, by)
            send_rows(k, bx, by)

        late = k - RELAY_LAG
        ox = pick(late, [o[0] for o in ORDER])
        oy = pick(late, [o[1] for o in ORDER])
        live = (late >= 0) & (late < len(ORDER))

        @pl.when(live & (ox == far))
        def _():
            relay_rows(0, wrap(y + oy))

        @pl.when(live & (oy == far))
        def _():
            relay_rows(1, wrap(x + ox))

        for at, f, d in SUMS:
            @pl.when(k == at)
            def _():
                total = sums(f, d)
                if d == 0:
                    pown[f] = total
                else:
                    psend[f, d - 1] = total
                    send_sums(f, d)

        for at, f in SUM_RELAYS:
            @pl.when(k == at)
            def _():
                relay_sums(f)

        return carry

    lax.fori_loop(0, len(ORDER), step, 0)
    outs = [pltpu.make_async_copy(a, b, out_sem.at[i]) for i, (a, b) in enumerate(((dw1, dw1_ref), (dw3, dw3_ref), (dw2, dw2_ref)))]
    for cp in outs:
        cp.start()
    lax.fori_loop(len(ORDER), STEPS, step, 0)

    for f in (0, 1):
        total = pown[f]
        for d in range(1, side):
            if d == far:
                for i in (0, 1):
                    dst, sem = far_sum(f, i)
                    pltpu.make_async_copy(dst, dst, sem).wait()
            else:
                ref = precv.at[f, d - 1]
                pltpu.make_async_copy(ref, ref, p_recv.at[f, d - 1]).wait()
            total = total + precv[f, d - 1]
        dx_ref[:, f * half:(f + 1) * half] = total.astype(BF16)

    def drained(ref, sem):
        pltpu.make_async_copy(ref, ref, sem).wait()

    chips = side * side
    drained(dyall.at[pl.ds(0, 2 * chips - 1)], ag_send)
    drained(tab.at[pl.ds(0, 2 * chips - 1)], tb_send)
    drained(dxs.at[:, pl.ds(0, 2 * chips - side)], r_send)
    drained(dxs.at[:, pl.ds(0, 2 * side)], rl_send)
    drained(psend, p_send)
    drained(prelay, pl_send)
    for cp in outs:
        cp.wait()


def dgates_kernel(dy_ref, yb_ref, out_ref):
    out_ref[...] = jnp.sum(dy_ref[...].astype(F32)[:, None, :] * yb_ref[...].astype(F32), axis=2)


def solution(mesh):
    ep_size = mesh.shape['ep']
    side = math.isqrt(ep_size // 2)
    tok_spec = P(('dp', 'ep'), None)
    buf_spec = P(('dp', 'ep'), None, None)
    expert_spec = P('ep', None, None)

    def device_step(dy, topk_idx, slot_idx, gates, y_back, x_disp, h1_disp, h3_disp, w_gate, w_up, w_down):
        capacity = x_disp.shape[1] // ep_size
        tokens, d = dy.shape
        top = gates.shape[1]
        ff = w_gate.shape[2]
        half = d // 2
        rows = 2 * capacity
        row_len = 2 * side

        code = jnp.where(slot_idx >= 0, topk_idx * capacity + slot_idx, -1).astype(F32)
        tab = jnp.concatenate([code, gates], axis=1).T

        tb = min(32, tokens)
        d_gates = pl.pallas_call(
            dgates_kernel, grid=(tokens // tb,),
            in_specs=[pl.BlockSpec((tb, d), lambda i: (i, 0)), pl.BlockSpec((tb, top, d), lambda i: (i, 0, 0))],
            out_specs=pl.BlockSpec((tb, top), lambda i: (i, 0)),
            out_shape=jax.ShapeDtypeStruct((tokens, top), F32), name='dgates',
        )(dy, y_back)

        vm = pltpu.VMEM
        dma = pltpu.SemaphoreType.DMA
        any_spec = pl.BlockSpec(memory_space=pl.ANY)
        dx, dw1, dw3, dw2 = pl.pallas_call(
            functools.partial(kernel_body, side, capacity),
            in_specs=[any_spec] * 8,
            out_specs=[pl.BlockSpec(memory_space=pltpu.VMEM)] + [any_spec] * 3,
            out_shape=[jax.ShapeDtypeStruct((tokens, d), BF16),
                       jax.ShapeDtypeStruct((d, ff), F32), jax.ShapeDtypeStruct((d, ff), F32),
                       jax.ShapeDtypeStruct((ff, d), F32)],
            scratch_shapes=[
                vm((ep_size, 2, tokens, half), BF16), vm((ep_size, 2 * top, tokens), F32),
                vm((d, ff), BF16), vm((d, ff), BF16), vm((ff, d), BF16),
                vm((d, ff), F32), vm((d, ff), F32), vm((ff, d), F32),
                vm((2, rows, d), BF16), vm((2, rows, ff), BF16), vm((2, rows, ff), BF16),
                vm((rows, d), BF16), vm((rows, 2 * ff), BF16),
                vm((2, ep_size, capacity, half), BF16),
                vm((2, side * row_len + 2 * side, capacity, half), BF16),
                vm((row_len * capacity, tokens), BF16),
                vm((2, side - 1, tokens, half), F32), vm((2, tokens, half), F32),
                vm((2, side - 1, tokens, half), F32), vm((2, 2, tokens // 2, half), F32),
                dma((3,)), dma((3,)), dma((2, 3)), dma((3,)),
                dma, dma((side * side, 2, 2)), dma((side * side, 2, 2)),
                dma, dma((side * side, 2)), dma((side * side, 2)),
                dma, dma((2, side * row_len + 2 * side)), dma,
                dma, dma((2, side)), dma, dma((2, 2)),
            ],
            compiler_params=pltpu.CompilerParams(collective_id=0, has_side_effects=True, vmem_limit_bytes=67043328),
            name='moe_bwd',
        )(dy, tab, x_disp[0], h1_disp[0], h3_disp[0], w_gate[0], w_up[0], w_down[0])
        return dx, d_gates, dw1[None], dw3[None], dw2[None]

    return jax.shard_map(
        device_step, mesh=mesh,
        in_specs=(tok_spec, tok_spec, tok_spec, tok_spec, buf_spec, buf_spec, buf_spec, buf_spec,
                  expert_spec, expert_spec, expert_spec),
        out_specs=(tok_spec, tok_spec, buf_spec, buf_spec, buf_spec),
        check_vma=False)
```

time: 462 us -> 155 us (0.34); the launches traced: 454 us -> 154 us
  Pallas kernels: 0 us -> 143 us
  local copies, waits for them, and re-layouts: 144 us -> 8.38 us
  blocking collectives: 111 us -> 0 us
  matrix products: 66.5 us -> 0 us
  waiting for transfers between devices: 65.6 us -> 0 us
  other arithmetic: 60.7 us -> 2.02 us
  starting transfers between devices: 4.81 us -> 0 us
    pallas_call x0 -> x2, Pallas kernels: none -> 143 us  [the longest x1 136 us: device_step(): pl.pallas_call(functools.partial(kernel_body, side, capacity), in_specs=[...]
    all_to_all x1 -> x0, blocking collectives: 111 us -> none  [device_step(): dy_disp = lax.all_to_all(send_buf, 'ep', 0, 1, tiled=True)]
    dot_general x7 -> x0, matrix products: 66.5 us -> none  [the longest x1 11.9 us: expert_backward(): jnp.einsum('erf,erd->efd', hidden_act, dy_disp, preferred_element_type=jn...]
    all_to_all x1 -> x0, waiting for transfers between devices: 65.6 us -> none  [device_step(): lax.all_to_all(dx_disp, 'ep', 1, 0, tiled=True).reshape(rows_all, d_model)]
    gather x3 -> x0, local copies, waits for them, and re-layouts: 56.7 us -> none  [the longest x1 23 us: gated_buffer(): row_gate = gate_pad[choice_of]]
    unnamed x23 -> x13, local copies, waits for them, and re-layouts: 62.1 us -> 8.38 us
    unnamed x1 -> x0, other arithmetic: 49.7 us -> none
    convert_element_type x1 -> x0, local copies, waits for them, and re-layouts: 15.5 us -> none  [expert_backward(): dx_disp = (jnp.einsum('erf,edf->erd', dh_gate, w_gate, preferred_element_...]
  transfers between devices with their start and end apart: 1 -> 0, of which waited for: 1 -> 0; matrix products, arithmetic and copies ran while one was open for 9% -> 0% of each run, Pallas kernels for 0% -> 0%
where the time goes in v2:
time: 155 us; the launch traced here: 154 us
  Pallas kernels  143 us (92%)
  local copies, waits for them, and re-layouts  8.38 us (5%)
  other arithmetic  2.02 us (1%)
    pallas_call x1, Pallas kernels, device_step(): pl.pallas_call(functools.partial(kernel_body, side, capacity), in_specs=[...  136 us
    unnamed x13, local copies, waits for them, and re-layouts  8.38 us
    pallas_call x1, Pallas kernels, device_step(): pl.pallas_call(dgates_kernel, grid=(tokens // tb,), in_specs=[pl.BlockSpe...  6.76 us

profile of v2, /device:TPU:97, one launch (start us, length us, event | category | flops | bytes accessed | tf_op | source)
XLA Modules:
  0.0 154.3 jit_solution(4786422459745725477)
XLA Ops:
  0.6 0.7 select_convert_fusion
  1.4 1.3 maximum_bitcast_fusion.tab_in
  2.7 136.5 %moe_bwd.1 = (bf16[256,1024]{1,0:T(8,128)(2,1)}, f32[1024,512]{1,0:T(8,128)}, f32[1024,512]{1,0:T(8,128)}, f32[512,1024]{1,0:T(8,128)}) custom-call(bf16[256,1024]{1,0:T(8,128)(2,1)} %dy_ref.3, f32[16,256]{1,0:T(8,128)} %maximum_bitcast_fusion.tab_in, bf16[4096,1024]{1,0:T(8,128)(2,1)} %bitcast.11, bf16[4096,512]{1,0:T(8,128)(2,1)} %bitcast.12, ...), custom_call_target="tpu_custom_call" | custom-call | tf_op jit(solution)/shard_map/moe_bwd/pallas_call | solution.py:417
  139.1 0.0 copy-start.3
  139.2 0.0 copy-start.2
  139.2 6.8 %dgates.1 = f32[256,8]{1,0:T(8,128)} custom-call(bf16[256,1024]{1,0:T(8,128)(2,1)} %dy_ref.3, bf16[256,8,1024]{2,1,0:T(8,128)(2,1)} %yb_ref.1), custom_call_target="tpu_custom_call" | custom-call | tf_op jit(solution)/shard_map/dgates/pallas_call | solution.py:407
  145.9 1.6 %copy.16 = f32[256,8]{0,1:T(8,128)} copy(f32[256,8]{1,0:T(8,128)} %dgates.1) | data formatting | bytes 16384
  147.5 0.0 copy-done.3
  147.5 0.8 copy.21
  148.3 0.0 copy-done.2
  148.3 0.0 copy-start.1
  148.3 1.3 copy.22
  149.6 1.0 copy-done.1
  150.7 0.0 copy-start
  150.7 1.3 copy.23
  152.0 1.0 copy-done
  153.0 1.3 copy.24
Async XLA Ops:
  139.1 8.4 %copy-start.3 = (bf16[256,1024]{1,0:T(8,128)(2,1)S(1)}, bf16[256,1024]{1,0:T(8,128)(2,1)}, u32[]{:S(2)}) copy-start(bf16[256,1024]{1,0:T(8,128)(2,1)} %get-tuple-element.23) | copy-start | bytes 1572868
  139.2 9.1 %copy-start.2 = (f32[1024,512]{1,0:T(8,128)S(1)}, f32[1024,512]{1,0:T(8,128)}, u32[]{:S(2)}) copy-start(f32[1024,512]{1,0:T(8,128)} %get-tuple-element.10) | copy-start | bytes 6291460
  148.3 2.3 %copy-start.1 = (f32[1024,512]{1,0:T(8,128)S(1)}, f32[1024,512]{1,0:T(8,128)}, u32[]{:S(2)}) copy-start(f32[1024,512]{1,0:T(8,128)} %get-tuple-element.11) | copy-start | bytes 6291460
  150.7 2.3 %copy-start = (f32[512,1024]{1,0:T(8,128)S(1)}, f32[512,1024]{1,0:T(8,128)}, u32[]{:S(2)}) copy-start(f32[512,1024]{1,0:T(8,128)} %get-tuple-element.12) | copy-start | bytes 6291460

commit v3 on v2

--- a/solution.py
+++ b/solution.py
@@ -14,8 +14,6 @@
 ORDER = ((2, 2), (2, 1), (1, 2), (2, 3), (3, 2), (2, 0), (0, 2),
          (1, 1), (1, 3), (3, 1), (1, 0), (0, 1), (3, 3), (3, 0), (0, 3), (0, 0))
 SUMS = ((8, 1, 2), (9, 0, 2), (13, 1, 1), (14, 0, 1), (16, 1, 3), (17, 0, 3), (18, 1, 0), (19, 0, 0))
-RELAY_LAG = 2
-SUM_RELAYS = ((12, 1), (13, 0))
 STEPS = 20
 
 
@@ -30,12 +28,12 @@
     return out
 
 
-def kernel_body(side, capacity, dy_ref, tab_in, x_ref, h1_ref, h3_ref, w1_ref, w3_ref, w2_ref,
-                dx_ref, dw1_ref, dw3_ref, dw2_ref,
-                dyall, tab, w1, w3, w2, dw1, dw3, dw2, xb, h1b, h3b, dyd, dh, dxs, rcv, hitb,
+def kernel_body(side, capacity, dy_ref, topk_ref, slot_ref, gates_ref, yb_ref, x_ref, h1_ref, h3_ref, w1_ref, w3_ref, w2_ref,
+                dx_ref, dg_ref, dw1_ref, dw3_ref, dw2_ref,
+                dyall, tab, w1, w3, w2, dw1, dw3, dw2, xb, h1b, h3b, dyd, dh, dxs, rcv, hitb, topk, slots, yb, dg,
                 psend, pown, precv, prelay,
-                load_sem, w_sem, in_sem, out_sem, ag_send, ag_recv, ag_recv2, tb_send, tb_recv, tb_recv2,
-                r_send, r_recv, rl_send, p_send, p_recv, pl_send, pl_recv):
+                load_sem, w_sem, yb_sem, in_sem, out_sem, ag_send, ag_recv, ag_recv2, tb_send, tb_recv, tb_recv2,
+                r_send, r_recv, p_send, p_recv, pl_recv):
     tokens = dyall.shape[2]
     top = tab.shape[1] // 2
     half = dyall.shape[3]
@@ -62,9 +60,16 @@
         return (wrap(x + r1), wrap(y + r2)) if f == 0 else (wrap(x + r2), wrap(y + r1))
 
     loads = [pltpu.make_async_copy(dy_ref.at[:, pl.ds(f * half, half)], dyall.at[me, f], load_sem.at[f]) for f in (0, 1)]
-    loads.append(pltpu.make_async_copy(tab_in, tab.at[me], load_sem.at[2]))
+    loads += [pltpu.make_async_copy(a, b, load_sem.at[2 + i]) for i, (a, b) in enumerate((
+        (topk_ref, topk), (slot_ref, slots), (gates_ref, tab.at[me, pl.ds(top, top)])))]
     wloads = [pltpu.make_async_copy(a, b, w_sem.at[i]) for i, (a, b) in enumerate(((w1_ref, w1), (w3_ref, w3), (w2_ref, w2)))]
     for cp in loads + wloads:
+        cp.start()
+
+    chunk = yb.shape[1]
+    yb_loads = [pltpu.make_async_copy(yb_ref.at[pl.ds(i * chunk, chunk)], yb.at[i % 2], yb_sem.at[i % 2])
+                for i in range(tokens // chunk)]
+    for cp in yb_loads[:2]:
         cp.start()
 
     def stream(k):
@@ -79,11 +84,15 @@
         cp.start()
 
     barrier = pltpu.get_barrier_semaphore()
+    peers = [(wrap(x + r), y) for r in range(1, side)] + [(x, wrap(y + r)) for r in range(1, side)]
     for c in (0, 1):
-        for bx, by in ((wrap(x + 1), y), (wrap(x - 1), y), (x, wrap(y + 1)), (x, wrap(y - 1))):
+        for bx, by in peers:
             pl.semaphore_signal(barrier, inc=1, device_id=device(bx, by, c))
     pl.semaphore_signal(barrier, inc=1, device_id=device(x, y, 1 - core))
-    pl.semaphore_wait(barrier, 9)
+    for cp in loads:
+        cp.wait()
+    tab[me, 0:top, :] = jnp.where(slots[...] >= 0, topk[...] * capacity + slots[...], -1).astype(F32)
+    pl.semaphore_wait(barrier, 2 * len(peers) + 1)
 
     def gather_copy(f, p, r1, r2, axis, sign):
         bx, by = chip(f, r1, r2)
@@ -108,8 +117,6 @@
         for cp in gather_copy(f, p, r1, r2, 0, 1):
             cp.wait_recv()
 
-    for cp in loads:
-        cp.wait()
     for axis in (0, 1):
         for f in (0, 1):
             for p, sign in ((0, 1), (1, -1), (1, 1), (0, -1)):
@@ -157,19 +164,26 @@
                 arrived(f, p, r1, far)
                 send(f, p, r1, far, None)
 
+    def gate_grads(i):
+        yb_loads[i].wait()
+        part = sum(jnp.sum(dyall[me, f, i * chunk:(i + 1) * chunk, :].astype(F32)[:, None, :]
+                           * yb[i % 2, :, :, f * half:(f + 1) * half].astype(F32), axis=2) for f in (0, 1))
+        dg[i * chunk:(i + 1) * chunk, 0:top] = part
+        if i + 2 < len(yb_loads):
+            yb_loads[i + 2].start()
+
     first_near()
     dw1[...] = jnp.zeros_like(dw1)
     dw3[...] = jnp.zeros_like(dw3)
     dw2[...] = jnp.zeros_like(dw2)
-    second_near(0)
-    first_far()
-    second_far(0)
-    second_near(-1)
-    second_near(1)
-    second_near(far)
-    second_far(-1)
-    second_far(1)
-    second_far(far)
+    dg[...] = jnp.zeros_like(dg)
+    groups = [(second_near, 0), (first_far,), (second_far, 0), (second_near, -1), (second_near, 1),
+              (second_near, far), (second_far, -1), (second_far, 1), (second_far, far)]
+    for i, group in enumerate(groups):
+        group[0](*group[1:])
+        if i < len(yb_loads):
+            gate_grads(i)
+    dg_ref[...] = dg[...].T[0:top, :]
 
     def plane(b, carry):
         home = b * 2 + 1 - core
@@ -238,35 +252,19 @@
             d = pick(k, [o[f] for o in ORDER])
             pos = x if f == 0 else y
             other = by if f == 0 else bx
-            slot_near = other * row_len + pos * 2 + core
+            slot = other * row_len + pos * 2 + core
             for cc in (0, 1):
                 home = block(bx, by) * 2 + cc
-                same = core == cc
-                local = (d == 0) & same
+                local = (d == 0) & (core == cc)
 
                 @pl.when(local)
                 def _():
-                    rcv[f, slot_near] = dxs[f, home]
+                    rcv[f, slot] = dxs[f, home]
 
                 @pl.when(jnp.logical_not(local))
                 def _():
-                    plus = (d == 1) | ((d == far) & same)
-                    sign = jnp.where(d == 0, 0, jnp.where(plus, 1, -1))
-                    slot = jnp.where(d == far, side * row_len + jnp.where(same, 0, side) + other, slot_near)
                     pltpu.make_async_remote_copy(dxs.at[f, home], rcv.at[f, slot], r_send, r_recv.at[f, slot],
-                                                 device_id=target(f, sign, cc)).start()
-
-    def relay_rows(f, other):
-        pos = x if f == 0 else y
-        for sign in (1, -1):
-            slot_in = side * row_len + (0 if sign == 1 else side) + other
-            src_core = core if sign == 1 else 1 - core
-            slot_out = other * row_len + wrap(pos - sign) * 2 + src_core
-            cp = pltpu.make_async_remote_copy(rcv.at[f, slot_in], rcv.at[f, slot_out], rl_send,
-                                              r_recv.at[f, slot_in], device_id=target(f, sign, core))
-            cp.wait_recv()
-            pltpu.make_async_remote_copy(rcv.at[f, slot_in], rcv.at[f, slot_out], rl_send,
-                                         r_recv.at[f, slot_out], device_id=target(f, sign, core)).start()
+                                                 device_id=target(f, d, cc)).start()
 
     def sums(f, d):
         pos = x if f == 0 else y
@@ -288,26 +286,21 @@
         data = rcv[f, pl.ds(other * row_len, row_len)].reshape(row_len * capacity, half)
         return mm(hitb[...], data, ((0,), (0,)))
 
-    def send_sums(f, d):
+    def send_sums(f, d, total):
         axis = 1 - f
         if d == far:
+            psend[f, d - 1] = total
             for i, sign in ((0, 1), (1, -1)):
                 pltpu.make_async_remote_copy(psend.at[f, d - 1, pl.ds(i * piece, piece)], prelay.at[f, i], p_send,
                                              pl_recv.at[f, i], device_id=target(axis, sign, core)).start()
         else:
-            sign = 1 if d == 1 else -1
-            pltpu.make_async_remote_copy(psend.at[f, d - 1], precv.at[f, d - 1], p_send, p_recv.at[f, d - 1],
-                                         device_id=target(axis, sign, core)).start()
-
-    def far_sum(f, i):
-        return precv.at[f, far - 1, pl.ds(i * piece, piece)], p_recv.at[f, far - 1 if i == 0 else side - 1]
-
-    def relay_sums(f):
-        for i, sign in ((0, 1), (1, -1)):
+            i, sign = (0, 1) if d == 1 else (1, -1)
             src = prelay.at[f, i]
             pltpu.make_async_copy(src, src, pl_recv.at[f, i]).wait()
-            dst, sem = far_sum(f, i)
-            pltpu.make_async_remote_copy(src, dst, pl_send, sem, device_id=target(1 - f, sign, core)).start()
+            psend[f, d - 1] = total
+            psend[f, d - 1, i * piece:(i + 1) * piece, :] = total[i * piece:(i + 1) * piece, :] + prelay[f, i]
+            pltpu.make_async_remote_copy(psend.at[f, d - 1], precv.at[f, i], p_send, p_recv.at[f, i],
+                                         device_id=target(axis, sign, core)).start()
 
     def step(k, carry):
         @pl.when(k < len(ORDER))
@@ -317,19 +310,6 @@
             compute(k, bx, by)
             send_rows(k, bx, by)
 
-        late = k - RELAY_LAG
-        ox = pick(late, [o[0] for o in ORDER])
-        oy = pick(late, [o[1] for o in ORDER])
-        live = (late >= 0) & (late < len(ORDER))
-
-        @pl.when(live & (ox == far))
-        def _():
-            relay_rows(0, wrap(y + oy))
-
-        @pl.when(live & (oy == far))
-        def _():
-            relay_rows(1, wrap(x + ox))
-
         for at, f, d in SUMS:
             @pl.when(k == at)
             def _():
@@ -337,13 +317,7 @@
                 if d == 0:
                     pown[f] = total
                 else:
-                    psend[f, d - 1] = total
-                    send_sums(f, d)
-
-        for at, f in SUM_RELAYS:
-            @pl.when(k == at)
-            def _():
-                relay_sums(f)
+                    send_sums(f, d, total)
 
         return carry
 
@@ -355,15 +329,10 @@
 
     for f in (0, 1):
         total = pown[f]
-        for d in range(1, side):
-            if d == far:
-                for i in (0, 1):
-                    dst, sem = far_sum(f, i)
-                    pltpu.make_async_copy(dst, dst, sem).wait()
-            else:
-                ref = precv.at[f, d - 1]
-                pltpu.make_async_copy(ref, ref, p_recv.at[f, d - 1]).wait()
-            total = total + precv[f, d - 1]
+        for i in (0, 1):
+            ref = precv.at[f, i]
+            pltpu.make_async_copy(ref, ref, p_recv.at[f, i]).wait()
+            total = total + precv[f, i]
         dx_ref[:, f * half:(f + 1) * half] = total.astype(BF16)
 
     def drained(ref, sem):
@@ -373,15 +342,9 @@
     drained(dyall.at[pl.ds(0, 2 * chips - 1)], ag_send)
     drained(tab.at[pl.ds(0, 2 * chips - 1)], tb_send)
     drained(dxs.at[:, pl.ds(0, 2 * chips - side)], r_send)
-    drained(dxs.at[:, pl.ds(0, 2 * side)], rl_send)
     drained(psend, p_send)
-    drained(prelay, pl_send)
     for cp in outs:
         cp.wait()
-
-
-def dgates_kernel(dy_ref, yb_ref, out_ref):
-    out_ref[...] = jnp.sum(dy_ref[...].astype(F32)[:, None, :] * yb_ref[...].astype(F32), axis=2)
 
 
 def solution(mesh):
@@ -400,25 +363,15 @@
         rows = 2 * capacity
         row_len = 2 * side
 
-        code = jnp.where(slot_idx >= 0, topk_idx * capacity + slot_idx, -1).astype(F32)
-        tab = jnp.concatenate([code, gates], axis=1).T
-
-        tb = min(32, tokens)
-        d_gates = pl.pallas_call(
-            dgates_kernel, grid=(tokens // tb,),
-            in_specs=[pl.BlockSpec((tb, d), lambda i: (i, 0)), pl.BlockSpec((tb, top, d), lambda i: (i, 0, 0))],
-            out_specs=pl.BlockSpec((tb, top), lambda i: (i, 0)),
-            out_shape=jax.ShapeDtypeStruct((tokens, top), F32), name='dgates',
-        )(dy, y_back)
-
+        chunk = tokens // 8
         vm = pltpu.VMEM
         dma = pltpu.SemaphoreType.DMA
         any_spec = pl.BlockSpec(memory_space=pl.ANY)
-        dx, dw1, dw3, dw2 = pl.pallas_call(
+        dx, d_gates, dw1, dw3, dw2 = pl.pallas_call(
             functools.partial(kernel_body, side, capacity),
-            in_specs=[any_spec] * 8,
-            out_specs=[pl.BlockSpec(memory_space=pltpu.VMEM)] + [any_spec] * 3,
-            out_shape=[jax.ShapeDtypeStruct((tokens, d), BF16),
+            in_specs=[any_spec] * 11,
+            out_specs=[pl.BlockSpec(memory_space=pltpu.VMEM)] * 2 + [any_spec] * 3,
+            out_shape=[jax.ShapeDtypeStruct((tokens, d), BF16), jax.ShapeDtypeStruct((top, tokens), F32),
                        jax.ShapeDtypeStruct((d, ff), F32), jax.ShapeDtypeStruct((d, ff), F32),
                        jax.ShapeDtypeStruct((ff, d), F32)],
             scratch_shapes=[
@@ -428,20 +381,22 @@
                 vm((2, rows, d), BF16), vm((2, rows, ff), BF16), vm((2, rows, ff), BF16),
                 vm((rows, d), BF16), vm((rows, 2 * ff), BF16),
                 vm((2, ep_size, capacity, half), BF16),
-                vm((2, side * row_len + 2 * side, capacity, half), BF16),
+                vm((2, side * row_len, capacity, half), BF16),
                 vm((row_len * capacity, tokens), BF16),
+                vm((top, tokens), jnp.int32), vm((top, tokens), jnp.int32),
+                vm((2, chunk, top, d), BF16), vm((tokens, 128), F32),
                 vm((2, side - 1, tokens, half), F32), vm((2, tokens, half), F32),
-                vm((2, side - 1, tokens, half), F32), vm((2, 2, tokens // 2, half), F32),
-                dma((3,)), dma((3,)), dma((2, 3)), dma((3,)),
+                vm((2, 2, tokens, half), F32), vm((2, 2, tokens // 2, half), F32),
+                dma((5,)), dma((3,)), dma((2,)), dma((2, 3)), dma((3,)),
                 dma, dma((side * side, 2, 2)), dma((side * side, 2, 2)),
                 dma, dma((side * side, 2)), dma((side * side, 2)),
-                dma, dma((2, side * row_len + 2 * side)), dma,
-                dma, dma((2, side)), dma, dma((2, 2)),
+                dma, dma((2, side * row_len)),
+                dma, dma((2, 2)), dma((2, 2)),
             ],
             compiler_params=pltpu.CompilerParams(collective_id=0, has_side_effects=True, vmem_limit_bytes=67043328),
             name='moe_bwd',
-        )(dy, tab, x_disp[0], h1_disp[0], h3_disp[0], w_gate[0], w_up[0], w_down[0])
-        return dx, d_gates, dw1[None], dw3[None], dw2[None]
+        )(dy, topk_idx.T, slot_idx.T, gates.T, y_back, x_disp[0], h1_disp[0], h3_disp[0], w_gate[0], w_up[0], w_down[0])
+        return dx, d_gates.T, dw1[None], dw3[None], dw2[None]
 
     return jax.shard_map(
         device_step, mesh=mesh,

time: 155 us -> 140 us (0.903)
  Pallas kernels: 143 us -> 130 us
  other arithmetic: 2.02 us -> 0 us
  local copies, waits for them, and re-layouts: 8.38 us -> 10.1 us
    pallas_call x1, Pallas kernels: 136 us -> 130 us  [device_step(): pl.pallas_call(functools.partial(kernel_body, side, capacity), in_specs=[...]
    pallas_call x1 -> x0, Pallas kernels: 6.76 us -> none  [device_step(): pl.pallas_call(dgates_kernel, grid=(tokens // tb,), in_specs=[pl.BlockSpe...]
    unnamed x13 -> x9, local copies, waits for them, and re-layouts: 8.38 us -> 10.1 us
where the time goes in v3:
time: 140 us
  Pallas kernels  130 us (93%)
  local copies, waits for them, and re-layouts  10.1 us (7%)
    pallas_call x1, Pallas kernels, device_step(): pl.pallas_call(functools.partial(kernel_body, side, capacity), in_specs=[...  130 us
    unnamed x9, local copies, waits for them, and re-layouts  10.1 us

profile of v3, /device:TPU:97, one launch (start us, length us, event | category | flops | bytes accessed | tf_op | source)
XLA Modules:
  0.0 140.2 jit_solution(9991228741137927398)
XLA Ops:
  0.6 129.5 %moe_bwd.1 = (bf16[256,1024]{1,0:T(8,128)(2,1)}, f32[8,256]{1,0:T(8,128)}, f32[1024,512]{1,0:T(8,128)}, f32[1024,512]{1,0:T(8,128)}, f32[512,1024]{1,0:T(8,128)}) custom-call(bf16[256,1024]{1,0:T(8,128)(2,1)} %dy_ref.1, s32[8,256]{1,0:T(8,128)} %bitcast.22, s32[8,256]{1,0:T(8,128)} %bitcast.23, f32[8,256]{1,0:T(8,128)} %bitcast.24, ...), custom_call_target="tpu_custom_call" | custom-call | tf_op jit(solution)/shard_map/moe_bwd/pallas_call | solution.py:370
  130.2 1.9 %copy.21 = bf16[256,1024]{1,0:T(8,128)(2,1)} copy(bf16[256,1024]{1,0:T(8,128)(2,1)} %get-tuple-element.20) | data formatting | bytes 1048576
  132.0 1.3 copy.22
  133.3 0.0 copy-start.1
  133.3 3.2 %copy.23 = f32[1,1024,512]{2,1,0:T(8,128)} copy(f32[1,1024,512]{2,1,0:T(8,128)} %bitcast.18) | data formatting | bytes 4194304
  136.6 0.0 copy-done.1
  136.6 0.0 copy-start
  136.6 1.3 copy.24
  137.9 1.0 copy-done
  138.9 1.3 copy.25
Async XLA Ops:
  133.3 3.2 %copy-start.1 = (f32[1024,512]{1,0:T(8,128)S(1)}, f32[1024,512]{1,0:T(8,128)}, u32[]{:S(2)}) copy-start(f32[1024,512]{1,0:T(8,128)} %get-tuple-element.13) | copy-start | bytes 6291460
  136.6 2.3 %copy-start = (f32[512,1024]{1,0:T(8,128)S(1)}, f32[512,1024]{1,0:T(8,128)}, u32[]{:S(2)}) copy-start(f32[512,1024]{1,0:T(8,128)} %get-tuple-element.14) | copy-start | bytes 6291460

commit v4 on v3

--- a/solution.py
+++ b/solution.py
@@ -11,10 +11,16 @@
 F32 = jnp.float32
 BF16 = jnp.bfloat16
 
-ORDER = ((2, 2), (2, 1), (1, 2), (2, 3), (3, 2), (2, 0), (0, 2),
-         (1, 1), (1, 3), (3, 1), (1, 0), (0, 1), (3, 3), (3, 0), (0, 3), (0, 0))
-SUMS = ((8, 1, 2), (9, 0, 2), (13, 1, 1), (14, 0, 1), (16, 1, 3), (17, 0, 3), (18, 1, 0), (19, 0, 0))
-STEPS = 20
+ORDER = ((0, 0), (1, 0), (3, 0), (0, 1), (0, 3), (2, 0), (0, 2),
+         (1, 1), (3, 3), (1, 3), (3, 1), (2, 2), (2, 1), (1, 2), (2, 3), (3, 2))
+SENDS = ((0, 1, 2, 3, 4, 5, 6, 7, 8, -1, -1, 11, 12, 13, 14, 15, -1, -1, -1, -1, -1, -1, -1, -1),
+         (-1, -1, -1, -1, -1, -1, -1, -1, -1, -1, -1, -1, -1, -1, 9, 10, -1, -1, -1, -1, -1, -1, -1, -1))
+SUMS = ((9, 0, 0), (10, 1, 0), (16, 1, 2), (17, 0, 2), (18, 1, 1), (19, 0, 1), (20, 1, 3), (21, 0, 3))
+JOINS = ((22, 1), (23, 0))
+GROUPS = ((1, 'first_near'), (1, 'gates'), (1, 'second_near', 0), (3, 'first_far'), (4, 'second_near', -1),
+          (5, 'second_far', 0), (5, 'second_near', 1), (7, 'second_near', 2), (9, 'second_far', -1),
+          (10, 'second_far', 1), (11, 'second_far', 2))
+STEPS = 24
 
 
 def mm(a, b, dims):
@@ -172,20 +178,25 @@
         if i + 2 < len(yb_loads):
             yb_loads[i + 2].start()
 
-    first_near()
+    def gate_grads():
+        for i, load in enumerate(yb_loads):
+            load.wait()
+            part = sum(jnp.sum(dyall[me, f, i * chunk:(i + 1) * chunk, :].astype(F32)[:, None, :]
+                               * yb[i % 2, :, :, f * half:(f + 1) * half].astype(F32), axis=2) for f in (0, 1))
+            dg[i * chunk:(i + 1) * chunk, 0:top] = part
+            if i + 2 < len(yb_loads):
+                yb_loads[i + 2].start()
+        dg_ref[...] = dg[...].T[0:top, :]
+
+    run = {'first_near': first_near, 'first_far': first_far, 'second_near': second_near,
+           'second_far': second_far, 'gates': gate_grads}
+
     dw1[...] = jnp.zeros_like(dw1)
     dw3[...] = jnp.zeros_like(dw3)
     dw2[...] = jnp.zeros_like(dw2)
     dg[...] = jnp.zeros_like(dg)
-    groups = [(second_near, 0), (first_far,), (second_far, 0), (second_near, -1), (second_near, 1),
-              (second_near, far), (second_far, -1), (second_far, 1), (second_far, far)]
-    for i, group in enumerate(groups):
-        group[0](*group[1:])
-        if i < len(yb_loads):
-            gate_grads(i)
-    dg_ref[...] = dg[...].T[0:top, :]
-
-    def plane(b, carry):
+
+    def plane(b):
         home = b * 2 + 1 - core
         for f in (0, 1):
             for p in (0, 1):
@@ -194,14 +205,13 @@
         for p in (0, 1):
             t = tab.at[home, pl.ds(p * top, top)]
             pltpu.make_async_copy(t, t, tb_recv2.at[b, p]).wait()
-        return carry
-
-    lax.fori_loop(0, side * side, plane, 0)
+
     for cp in wloads:
         cp.wait()
 
     def compute(k, bx, by):
         s = k % 2
+        plane(block(bx, by))
         for cp in stream(k):
             cp.wait()
 
@@ -247,7 +257,9 @@
     def target(f, sign, c):
         return device(wrap(x + sign), y, c) if f == 0 else device(x, wrap(y + sign), c)
 
-    def send_rows(k, bx, by):
+    def send_rows(k):
+        bx = wrap(x + pick(k, [o[0] for o in ORDER]))
+        by = wrap(y + pick(k, [o[1] for o in ORDER]))
         for f in (0, 1):
             d = pick(k, [o[f] for o in ORDER])
             pos = x if f == 0 else y
@@ -295,20 +307,38 @@
                                              pl_recv.at[f, i], device_id=target(axis, sign, core)).start()
         else:
             i, sign = (0, 1) if d == 1 else (1, -1)
+            psend[f, d - 1] = total
+            part = pl.ds((1 - i) * piece, piece)
+            pltpu.make_async_remote_copy(psend.at[f, d - 1, part], precv.at[f, i, part], p_send, p_recv.at[f, i, 1 - i],
+                                         device_id=target(axis, sign, core)).start()
+
+    def join_sums(f):
+        for i, sign, d in ((0, 1, 1), (1, -1, side - 1)):
             src = prelay.at[f, i]
             pltpu.make_async_copy(src, src, pl_recv.at[f, i]).wait()
-            psend[f, d - 1] = total
-            psend[f, d - 1, i * piece:(i + 1) * piece, :] = total[i * piece:(i + 1) * piece, :] + prelay[f, i]
-            pltpu.make_async_remote_copy(psend.at[f, d - 1], precv.at[f, i], p_send, p_recv.at[f, i],
-                                         device_id=target(axis, sign, core)).start()
+            part = pl.ds(i * piece, piece)
+            psend[f, d - 1, part] = psend[f, d - 1, part] + prelay[f, i]
+            pltpu.make_async_remote_copy(psend.at[f, d - 1, part], precv.at[f, i, part], p_send, p_recv.at[f, i, i],
+                                         device_id=target(1 - f, sign, core)).start()
 
     def step(k, carry):
+        for at, name, *arg in GROUPS:
+            @pl.when(k == at)
+            def _():
+                run[name](*arg)
+
         @pl.when(k < len(ORDER))
         def _():
             bx = wrap(x + pick(k, [o[0] for o in ORDER]))
             by = wrap(y + pick(k, [o[1] for o in ORDER]))
             compute(k, bx, by)
-            send_rows(k, bx, by)
+
+        for sends in SENDS:
+            which = pick(k, sends)
+
+            @pl.when(which >= 0)
+            def _():
+                send_rows(which)
 
         for at, f, d in SUMS:
             @pl.when(k == at)
@@ -319,6 +349,11 @@
                 else:
                     send_sums(f, d, total)
 
+        for at, f in JOINS:
+            @pl.when(k == at)
+            def _():
+                join_sums(f)
+
         return carry
 
     lax.fori_loop(0, len(ORDER), step, 0)
@@ -330,8 +365,9 @@
     for f in (0, 1):
         total = pown[f]
         for i in (0, 1):
-            ref = precv.at[f, i]
-            pltpu.make_async_copy(ref, ref, p_recv.at[f, i]).wait()
+            for p in (0, 1):
+                ref = precv.at[f, i, pl.ds(p * piece, piece)]
+                pltpu.make_async_copy(ref, ref, p_recv.at[f, i, p]).wait()
             total = total + precv[f, i]
         dx_ref[:, f * half:(f + 1) * half] = total.astype(BF16)
 
@@ -391,7 +427,7 @@
                 dma, dma((side * side, 2, 2)), dma((side * side, 2, 2)),
                 dma, dma((side * side, 2)), dma((side * side, 2)),
                 dma, dma((2, side * row_len)),
-                dma, dma((2, 2)), dma((2, 2)),
+                dma, dma((2, 2, 2)), dma((2, 2)),
             ],
             compiler_params=pltpu.CompilerParams(collective_id=0, has_side_effects=True, vmem_limit_bytes=67043328),
             name='moe_bwd',

time: 140 us -> 132 us (0.943)
  Pallas kernels: 130 us -> 121 us
    pallas_call x1, Pallas kernels: 130 us -> 121 us  [device_step(): pl.pallas_call(functools.partial(kernel_body, side, capacity), in_specs=[...]
where the time goes in v4:
time: 132 us
  Pallas kernels  121 us (92%)
  local copies, waits for them, and re-layouts  10.1 us (8%)
    pallas_call x1, Pallas kernels, device_step(): pl.pallas_call(functools.partial(kernel_body, side, capacity), in_specs=[...  121 us
    unnamed x9, local copies, waits for them, and re-layouts  10.1 us

profile of v4, /device:TPU:97, one launch (start us, length us, event | category | flops | bytes accessed | tf_op | source)
XLA Modules:
  0.0 131.5 jit_solution(17672330272529147040)
XLA Ops:
  0.6 120.8 %moe_bwd.1 = (bf16[256,1024]{1,0:T(8,128)(2,1)}, f32[8,256]{1,0:T(8,128)}, f32[1024,512]{1,0:T(8,128)}, f32[1024,512]{1,0:T(8,128)}, f32[512,1024]{1,0:T(8,128)}) custom-call(bf16[256,1024]{1,0:T(8,128)(2,1)} %dy_ref.1, s32[8,256]{1,0:T(8,128)} %bitcast.22, s32[8,256]{1,0:T(8,128)} %bitcast.23, f32[8,256]{1,0:T(8,128)} %bitcast.24, ...), custom_call_target="tpu_custom_call" | custom-call | tf_op jit(solution)/shard_map/moe_bwd/pallas_call | solution.py:406
  121.5 1.9 %copy.21 = bf16[256,1024]{1,0:T(8,128)(2,1)} copy(bf16[256,1024]{1,0:T(8,128)(2,1)} %get-tuple-element.20) | data formatting | bytes 1048576
  123.3 1.3 copy.22
  124.6 0.0 copy-start.1
  124.6 3.2 %copy.23 = f32[1,1024,512]{2,1,0:T(8,128)} copy(f32[1,1024,512]{2,1,0:T(8,128)} %bitcast.18) | data formatting | bytes 4194304
  127.9 0.0 copy-done.1
  127.9 0.0 copy-start
  127.9 1.3 %copy.24 = f32[1,1024,512]{2,1,0:T(8,128)} copy(f32[1,1024,512]{2,1,0:T(8,128)S(1)} %bitcast.17) | data formatting | bytes 4194304
  129.2 1.0 copy-done
  130.2 1.3 %copy.25 = f32[1,512,1024]{2,1,0:T(8,128)} copy(f32[1,512,1024]{2,1,0:T(8,128)S(1)} %bitcast.16) | data formatting | bytes 4194304
Async XLA Ops:
  124.6 3.2 %copy-start.1 = (f32[1024,512]{1,0:T(8,128)S(1)}, f32[1024,512]{1,0:T(8,128)}, u32[]{:S(2)}) copy-start(f32[1024,512]{1,0:T(8,128)} %get-tuple-element.13) | copy-start | bytes 6291460
  127.9 2.3 %copy-start = (f32[512,1024]{1,0:T(8,128)S(1)}, f32[512,1024]{1,0:T(8,128)}, u32[]{:S(2)}) copy-start(f32[512,1024]{1,0:T(8,128)} %get-tuple-element.14) | copy-start | bytes 6291460

commit v5 on v4

--- a/solution.py
+++ b/solution.py
@@ -13,8 +13,7 @@
 
 ORDER = ((0, 0), (1, 0), (3, 0), (0, 1), (0, 3), (2, 0), (0, 2),
          (1, 1), (3, 3), (1, 3), (3, 1), (2, 2), (2, 1), (1, 2), (2, 3), (3, 2))
-SENDS = ((0, 1, 2, 3, 4, 5, 6, 7, 8, -1, -1, 11, 12, 13, 14, 15, -1, -1, -1, -1, -1, -1, -1, -1),
-         (-1, -1, -1, -1, -1, -1, -1, -1, -1, -1, -1, -1, -1, -1, 9, 10, -1, -1, -1, -1, -1, -1, -1, -1))
+SENDS = ((0, 1, 2, 3, 4, 5, 6, 7, 8, 9, 10, 11, 12, 13, 14, 15)+(-1,)*8, (-1,)*24)
 SUMS = ((9, 0, 0), (10, 1, 0), (16, 1, 2), (17, 0, 2), (18, 1, 1), (19, 0, 1), (20, 1, 3), (21, 0, 3))
 JOINS = ((22, 1), (23, 0))
 GROUPS = ((1, 'first_near'), (1, 'gates'), (1, 'second_near', 0), (3, 'first_far'), (4, 'second_near', -1),
@@ -35,10 +34,10 @@
 
 
 def kernel_body(side, capacity, dy_ref, topk_ref, slot_ref, gates_ref, yb_ref, x_ref, h1_ref, h3_ref, w1_ref, w3_ref, w2_ref,
-                dx_ref, dg_ref, dw1_ref, dw3_ref, dw2_ref,
-                dyall, tab, w1, w3, w2, dw1, dw3, dw2, xb, h1b, h3b, dyd, dh, dxs, rcv, hitb, topk, slots, yb, dg,
+                dx_ref, dg_ref, dw1, dw3, dw2,
+                dyall, tab, w1, w3, w2, xb, h1b, h3b, dyd, dh, dxs, rcv, hitb, topk, slots, yb, dg,
                 psend, pown, precv, prelay,
-                load_sem, w_sem, yb_sem, in_sem, out_sem, ag_send, ag_recv, ag_recv2, tb_send, tb_recv, tb_recv2,
+                load_sem, w_sem, yb_sem, in_sem, ag_send, ag_recv, ag_recv2, tb_send, tb_recv, tb_recv2,
                 r_send, r_recv, p_send, p_recv, pl_recv):
     tokens = dyall.shape[2]
     top = tab.shape[1] // 2
@@ -356,11 +355,7 @@
 
         return carry
 
-    lax.fori_loop(0, len(ORDER), step, 0)
-    outs = [pltpu.make_async_copy(a, b, out_sem.at[i]) for i, (a, b) in enumerate(((dw1, dw1_ref), (dw3, dw3_ref), (dw2, dw2_ref)))]
-    for cp in outs:
-        cp.start()
-    lax.fori_loop(len(ORDER), STEPS, step, 0)
+    lax.fori_loop(0, STEPS, step, 0)
 
     for f in (0, 1):
         total = pown[f]
@@ -379,8 +374,6 @@
     drained(tab.at[pl.ds(0, 2 * chips - 1)], tb_send)
     drained(dxs.at[:, pl.ds(0, 2 * chips - side)], r_send)
     drained(psend, p_send)
-    for cp in outs:
-        cp.wait()
 
 
 def solution(mesh):
@@ -406,14 +399,12 @@
         dx, d_gates, dw1, dw3, dw2 = pl.pallas_call(
             functools.partial(kernel_body, side, capacity),
             in_specs=[any_spec] * 11,
-            out_specs=[pl.BlockSpec(memory_space=pltpu.VMEM)] * 2 + [any_spec] * 3,
-            out_shape=[jax.ShapeDtypeStruct((tokens, d), BF16), jax.ShapeDtypeStruct((top, tokens), F32),
-                       jax.ShapeDtypeStruct((d, ff), F32), jax.ShapeDtypeStruct((d, ff), F32),
-                       jax.ShapeDtypeStruct((ff, d), F32)],
+            out_specs=[pl.BlockSpec(memory_space=pltpu.VMEM)] * 5,
+            out_shape=[vm((tokens, d), BF16), vm((top, tokens), F32),
+                       vm((d, ff), F32), vm((d, ff), F32), vm((ff, d), F32)],
             scratch_shapes=[
                 vm((ep_size, 2, tokens, half), BF16), vm((ep_size, 2 * top, tokens), F32),
                 vm((d, ff), BF16), vm((d, ff), BF16), vm((ff, d), BF16),
-                vm((d, ff), F32), vm((d, ff), F32), vm((ff, d), F32),
                 vm((2, rows, d), BF16), vm((2, rows, ff), BF16), vm((2, rows, ff), BF16),
                 vm((rows, d), BF16), vm((rows, 2 * ff), BF16),
                 vm((2, ep_size, capacity, half), BF16),
@@ -423,13 +414,13 @@
                 vm((2, chunk, top, d), BF16), vm((tokens, 128), F32),
                 vm((2, side - 1, tokens, half), F32), vm((2, tokens, half), F32),
                 vm((2, 2, tokens, half), F32), vm((2, 2, tokens // 2, half), F32),
-                dma((5,)), dma((3,)), dma((2,)), dma((2, 3)), dma((3,)),
+                dma((5,)), dma((3,)), dma((2,)), dma((2, 3)),
                 dma, dma((side * side, 2, 2)), dma((side * side, 2, 2)),
                 dma, dma((side * side, 2)), dma((side * side, 2)),
                 dma, dma((2, side * row_len)),
                 dma, dma((2, 2, 2)), dma((2, 2)),
             ],
-            compiler_params=pltpu.CompilerParams(collective_id=0, has_side_effects=True, vmem_limit_bytes=67043328),
+            compiler_params=pltpu.CompilerParams(collective_id=0, has_side_effects=True, vmem_limit_bytes=56 * 2 ** 20),
             name='moe_bwd',
         )(dy, topk_idx.T, slot_idx.T, gates.T, y_back, x_disp[0], h1_disp[0], h3_disp[0], w_gate[0], w_up[0], w_down[0])
         return dx, d_gates.T, dw1[None], dw3[None], dw2[None]

time: 132 us -> 125 us (0.947)
  local copies, waits for them, and re-layouts: 10.1 us -> 5.35 us
  Pallas kernels: 121 us -> 119 us
    unnamed x9 -> x5, local copies, waits for them, and re-layouts: 10.1 us -> 5.35 us
    pallas_call x1, Pallas kernels: 121 us -> 119 us  [device_step(): pl.pallas_call(functools.partial(kernel_body, side, capacity), in_specs=[...]
where the time goes in v5:
time: 125 us
  Pallas kernels  119 us (95%)
  local copies, waits for them, and re-layouts  5.35 us (4%)
    pallas_call x1, Pallas kernels, device_step(): pl.pallas_call(functools.partial(kernel_body, side, capacity), in_specs=[...  119 us
    unnamed x5, local copies, waits for them, and re-layouts  5.35 us

profile of v5, /device:TPU:97, one launch (start us, length us, event | category | flops | bytes accessed | tf_op | source)
XLA Modules:
  0.0 124.7 jit_solution(16249656942874478356)
XLA Ops:
  0.6 118.7 %moe_bwd.1 = (bf16[256,1024]{1,0:T(8,128)(2,1)S(1)}, f32[8,256]{1,0:T(8,128)S(1)}, f32[1024,512]{1,0:T(8,128)S(1)}, f32[1024,512]{1,0:T(8,128)S(1)}, f32[512,1024]{1,0:T(8,128)S(1)}) custom-call(bf16[256,1024]{1,0:T(8,128)(2,1)} %dy_ref.1, s32[8,256]{1,0:T(8,128)} %bitcast.23, s32[8,256]{1,0:T(8,128)} %bitcast.24, f32[8,256]{1,0:T(8,128)} %bitcast.25, ...), custom_call_target="tpu_custom_call" | custom-call | tf_op jit(solution)/shard_map/moe_bwd/pallas_call | solution.py:399
  119.4 0.8 copy.21
  120.2 0.6 copy.22
  120.8 1.3 %copy.23 = f32[1,1024,512]{2,1,0:T(8,128)} copy(f32[1,1024,512]{2,1,0:T(8,128)S(1)} %bitcast.15) | data formatting | bytes 4194304
  122.1 1.3 %copy.24 = f32[1,1024,512]{2,1,0:T(8,128)} copy(f32[1,1024,512]{2,1,0:T(8,128)S(1)} %bitcast.14) | data formatting | bytes 4194304
  123.4 1.3 %copy.25 = f32[1,512,1024]{2,1,0:T(8,128)} copy(f32[1,512,1024]{2,1,0:T(8,128)S(1)} %bitcast.13) | data formatting | bytes 4194304

commit v6 on v5

--- a/solution.py
+++ b/solution.py
@@ -282,20 +282,21 @@
         hx, hy = (x, wrap(y + d)) if f == 0 else (wrap(x + d), y)
         other = hy if f == 0 else hx
         home = block(hx, hy) * 2 + core
-        code = tab[home, 0:top, :]
-        slot_row = lax.broadcasted_iota(jnp.int32, (capacity, tokens), 0).astype(F32)
+        code = tab[home].T[:, 0:top]
+        slot_col = lax.broadcasted_iota(jnp.int32, (tokens, capacity), 1).astype(F32)
+        for s in range(row_len):
+            e = y * row_len + s if f == 0 else ((s // 2) * side + x) * 2 + s % 2
+            rel = code - (e * capacity).astype(F32)
+            slot = jnp.max(jnp.where((rel >= 0.0) & (rel < float(capacity)), rel, -1.0), axis=1, keepdims=True)
+            hitb[:, s * capacity:(s + 1) * capacity] = jnp.where(slot_col == slot, 1.0, 0.0).astype(BF16)
         for s in range(row_len):
             @pl.when(pos * 2 + core != s)
             def _():
                 ref = rcv.at[f, other * row_len + s]
                 pltpu.make_async_copy(ref, ref, r_recv.at[f, other * row_len + s]).wait()
 
-            e = y * row_len + s if f == 0 else ((s // 2) * side + x) * 2 + s % 2
-            rel = code - (e * capacity).astype(F32)
-            slot = jnp.max(jnp.where((rel >= 0.0) & (rel < float(capacity)), rel, -1.0), axis=0, keepdims=True)
-            hitb[s * capacity:(s + 1) * capacity, :] = jnp.where(slot_row == slot, 1.0, 0.0).astype(BF16)
         data = rcv[f, pl.ds(other * row_len, row_len)].reshape(row_len * capacity, half)
-        return mm(hitb[...], data, ((0,), (0,)))
+        return mm(hitb[...], data, ((1,), (0,)))
 
     def send_sums(f, d, total):
         axis = 1 - f
@@ -376,6 +377,15 @@
     drained(psend, p_send)
 
 
+def write_out(*refs):
+    n = (len(refs) - 1) // 2
+    copies = [pltpu.make_async_copy(refs[i], refs[n + i], refs[-1].at[i]) for i in range(n)]
+    for cp in copies:
+        cp.start()
+    for cp in copies:
+        cp.wait()
+
+
 def solution(mesh):
     ep_size = mesh.shape['ep']
     side = math.isqrt(ep_size // 2)
@@ -396,7 +406,7 @@
         vm = pltpu.VMEM
         dma = pltpu.SemaphoreType.DMA
         any_spec = pl.BlockSpec(memory_space=pl.ANY)
-        dx, d_gates, dw1, dw3, dw2 = pl.pallas_call(
+        kept = pl.pallas_call(
             functools.partial(kernel_body, side, capacity),
             in_specs=[any_spec] * 11,
             out_specs=[pl.BlockSpec(memory_space=pltpu.VMEM)] * 5,
@@ -409,7 +419,7 @@
                 vm((rows, d), BF16), vm((rows, 2 * ff), BF16),
                 vm((2, ep_size, capacity, half), BF16),
                 vm((2, side * row_len, capacity, half), BF16),
-                vm((row_len * capacity, tokens), BF16),
+                vm((tokens, row_len * capacity), BF16),
                 vm((top, tokens), jnp.int32), vm((top, tokens), jnp.int32),
                 vm((2, chunk, top, d), BF16), vm((tokens, 128), F32),
                 vm((2, side - 1, tokens, half), F32), vm((2, tokens, half), F32),
@@ -423,6 +433,14 @@
             compiler_params=pltpu.CompilerParams(collective_id=0, has_side_effects=True, vmem_limit_bytes=56 * 2 ** 20),
             name='moe_bwd',
         )(dy, topk_idx.T, slot_idx.T, gates.T, y_back, x_disp[0], h1_disp[0], h3_disp[0], w_gate[0], w_up[0], w_down[0])
+        dx, d_gates, dw1, dw3, dw2 = pl.pallas_call(
+            write_out,
+            in_specs=[pl.BlockSpec(memory_space=pltpu.VMEM)] * len(kept),
+            out_specs=[any_spec] * len(kept),
+            out_shape=[jax.ShapeDtypeStruct(a.shape, a.dtype) for a in kept],
+            scratch_shapes=[dma((len(kept),))], name='write_out',
+            compiler_params=pltpu.CompilerParams(vmem_limit_bytes=2 ** 20),
+        )(*[pltpu.with_memory_space_constraint(a, pltpu.VMEM) for a in kept])
         return dx, d_gates.T, dw1[None], dw3[None], dw2[None]
 
     return jax.shard_map(

time: 125 us -> 122 us (0.976)
  local copies, waits for them, and re-layouts: 5.35 us -> 0 us
  Pallas kernels: 119 us -> 122 us
    unnamed x5 -> x0, local copies, waits for them, and re-layouts: 5.35 us -> none
    pallas_call x0 -> x1, Pallas kernels: none -> 2.92 us  [device_step(): pl.pallas_call(write_out, in_specs=[pl.BlockSpec(memory_space=pltpu.VMEM)...]
where the time goes in v6:
time: 122 us
  Pallas kernels  122 us (100%)
    pallas_call x1, Pallas kernels, device_step(): pl.pallas_call(functools.partial(kernel_body, side, capacity), in_specs=[...  119 us
    pallas_call x1, Pallas kernels, device_step(): pl.pallas_call(write_out, in_specs=[pl.BlockSpec(memory_space=pltpu.VMEM)...  2.92 us

profile of v6, /device:TPU:97, one launch (start us, length us, event | category | flops | bytes accessed | tf_op | source)
XLA Modules:
  0.0 122.3 jit_solution(9587931960126574540)
XLA Ops:
  0.6 118.7 %moe_bwd.1 = (bf16[256,1024]{1,0:T(8,128)(2,1)S(1)}, f32[8,256]{1,0:T(8,128)S(1)}, f32[1024,512]{1,0:T(8,128)S(1)}, f32[1024,512]{1,0:T(8,128)S(1)}, f32[512,1024]{1,0:T(8,128)S(1)}) custom-call(bf16[256,1024]{1,0:T(8,128)(2,1)} %dy_ref.1, s32[8,256]{1,0:T(8,128)} %bitcast.19, s32[8,256]{1,0:T(8,128)} %bitcast.20, f32[8,256]{1,0:T(8,128)} %bitcast.21, ...), custom_call_target="tpu_custom_call" | custom-call | tf_op jit(solution)/shard_map/moe_bwd/pallas_call | solution.py:409
  119.4 2.9 %write_out.1 = (bf16[256,1024]{1,0:T(8,128)(2,1)}, f32[8,256]{1,0:T(8,128)}, f32[1024,512]{1,0:T(8,128)}, f32[1024,512]{1,0:T(8,128)}, f32[512,1024]{1,0:T(8,128)}) custom-call(bf16[256,1024]{1,0:T(8,128)(2,1)S(1)} %get-tuple-element.15.refs_0_, f32[8,256]{1,0:T(8,128)S(1)} %get-tuple-element.16.refs_1_, f32[1024,512]{1,0:T(8,128)S(1)} %get-tuple-element.17.refs_2_, ...), custom_call_target="tpu_custom_call" | custom-call | tf_op jit(solution)/shard_map/write_out/pallas_call | solution.py:436

commit v7 on v6

--- a/solution.py
+++ b/solution.py
@@ -89,15 +89,14 @@
         cp.start()
 
     barrier = pltpu.get_barrier_semaphore()
-    peers = [(wrap(x + r), y) for r in range(1, side)] + [(x, wrap(y + r)) for r in range(1, side)]
-    for c in (0, 1):
-        for bx, by in peers:
-            pl.semaphore_signal(barrier, inc=1, device_id=device(bx, by, c))
+    peers = [(wrap(x + 1), y), (wrap(x - 1), y), (x, wrap(y + 1)), (x, wrap(y - 1))]
+    for bx, by in peers:
+        pl.semaphore_signal(barrier, inc=1, device_id=device(bx, by, core))
     pl.semaphore_signal(barrier, inc=1, device_id=device(x, y, 1 - core))
     for cp in loads:
         cp.wait()
     tab[me, 0:top, :] = jnp.where(slots[...] >= 0, topk[...] * capacity + slots[...], -1).astype(F32)
-    pl.semaphore_wait(barrier, 2 * len(peers) + 1)
+    pl.semaphore_wait(barrier, len(peers) + 1)
 
     def gather_copy(f, p, r1, r2, axis, sign):
         bx, by = chip(f, r1, r2)
@@ -109,7 +108,7 @@
             nx, ny = chip(f, sign, 0) if axis == 0 else chip(f, 0, sign)
             dev, rs, ts = device(nx, ny, core), ag_recv, tb_recv
         out = [pltpu.make_async_remote_copy(src, src, ag_send, rs.at[block(bx, by), f, p], device_id=dev)]
-        if f == 0:
+        if f == p:
             t = tab.at[home, pl.ds(p * top, top)]
             out.append(pltpu.make_async_remote_copy(t, t, tb_send, ts.at[block(bx, by), p], device_id=dev))
         return out

time: 122 us -> 122 us (level)
  no operation moved by 1% of the time
where the time goes in v7:
time: 122 us
  Pallas kernels  121 us (99%)
    pallas_call x1, Pallas kernels, device_step(): pl.pallas_call(functools.partial(kernel_body, side, capacity), in_specs=[...  118 us
    pallas_call x1, Pallas kernels, device_step(): pl.pallas_call(write_out, in_specs=[pl.BlockSpec(memory_space=pltpu.VMEM)...  2.92 us

profile of v7, /device:TPU:97, one launch (start us, length us, event | category | flops | bytes accessed | tf_op | source)
XLA Modules:
  0.0 121.6 jit_solution(16673807278035480061)
XLA Ops:
  0.6 118.0 %moe_bwd.1 = (bf16[256,1024]{1,0:T(8,128)(2,1)S(1)}, f32[8,256]{1,0:T(8,128)S(1)}, f32[1024,512]{1,0:T(8,128)S(1)}, f32[1024,512]{1,0:T(8,128)S(1)}, f32[512,1024]{1,0:T(8,128)S(1)}) custom-call(bf16[256,1024]{1,0:T(8,128)(2,1)} %dy_ref.1, s32[8,256]{1,0:T(8,128)} %bitcast.19, s32[8,256]{1,0:T(8,128)} %bitcast.20, f32[8,256]{1,0:T(8,128)} %bitcast.21, ...), custom_call_target="tpu_custom_call" | custom-call | tf_op jit(solution)/shard_map/moe_bwd/pallas_call | solution.py:408
  118.7 2.9 %write_out.1 = (bf16[256,1024]{1,0:T(8,128)(2,1)}, f32[8,256]{1,0:T(8,128)}, f32[1024,512]{1,0:T(8,128)}, f32[1024,512]{1,0:T(8,128)}, f32[512,1024]{1,0:T(8,128)}) custom-call(bf16[256,1024]{1,0:T(8,128)(2,1)S(1)} %get-tuple-element.15.refs_0_, f32[8,256]{1,0:T(8,128)S(1)} %get-tuple-element.16.refs_1_, f32[1024,512]{1,0:T(8,128)S(1)} %get-tuple-element.17.refs_2_, ...), custom_call_target="tpu_custom_call" | custom-call | tf_op jit(solution)/shard_map/write_out/pallas_call | solution.py:435
